TPU v7x, 16 devices: a 4x2x1 block of a 4x4x8 slice. The times are simulated.
16 devices in a mesh: dp: 2 (over y, z), tp: 8 (over x, core).
Axes of the slice: x: 4, y: 2, z: 1, core: 2. Of those that a mesh axis runs over, the one named last changes fastest.
The devices are a block of a 4x4x8 slice.
Arguments:
- hidden: bfloat16 [512, 3, 4096], P(('dp', 'tp')), parts along dimension 0
- w_head: bfloat16 [4096, 32000], P(None, 'tp')
- q_draft: float32 [512, 2, 32000], P(('dp', 'tp')), parts along dimension 0
- draft_tok: int32 [512, 2], P('dp'), parts along dimension 0
Outputs:
- output 1: float32 [512, 2], P('dp'), parts along dimension 0
- output 2: float32 [512], P('dp'), parts along dimension 0
- output 3: float32 [512, 2, 32000], P('dp', None, 'tp'), parts along dimension 0
- output 4: float32 [512, 32000], P('dp', 'tp'), parts along dimension 0
There are 2 independent parts. A program takes and returns all parts, laid end to end along the dimension named above; an argument that names none is the same for every part.
All inputs are finite; a program needn't handle non-finite values.
Results may differ from a plain program's by a relative error of at most 0.001.
Values are sent between devices in bfloat16 or wider.
A program may use at most 768 MiB of HBM per device.

v0:
```python
import jax
import jax.numpy as jnp
from jax import lax
from jax.sharding import PartitionSpec as P

INV_TEMP = 1.25


def verify_local(hid_rows, w_cols, q_rows, draft_tok):
    shard_vocab = w_cols.shape[1]
    hid_all = lax.all_gather(hid_rows, 'tp', axis=0, tiled=True)
    logits = jnp.einsum('bgd,dv->bgv', hid_all, w_cols, preferred_element_type=jnp.float32) * INV_TEMP
    glob_max = lax.pmax(jnp.max(logits, axis=-1, keepdims=True), 'tp')
    exp_terms = jnp.exp(logits - glob_max)
    exp_total = lax.psum(jnp.sum(exp_terms, axis=-1, keepdims=True), 'tp')
    target_prob = exp_terms / exp_total
    draft_part = target_prob[:, :-1]
    q_cols = lax.all_to_all(q_rows, 'tp', 2, 0, tiled=True)
    local_ids = draft_tok - lax.axis_index('tp') * shard_vocab
    picker = local_ids[:, :, None] == jnp.arange(shard_vocab, dtype=jnp.int32)
    p_pick = jnp.sum(jnp.where(picker, draft_part, 0.0), axis=-1)
    q_pick = jnp.sum(jnp.where(picker, q_cols, 0.0), axis=-1)
    pick_pair = lax.psum(jnp.stack([p_pick, q_pick]), 'tp')
    accept = jnp.minimum(pick_pair[0] / pick_pair[1], 1.0)
    expected = jnp.sum(jnp.cumprod(accept, axis=1), axis=1)
    excess = jnp.maximum(draft_part - q_cols, 0.0)
    excess_mass = lax.psum(jnp.sum(excess, axis=-1, keepdims=True), 'tp')
    return accept, expected, excess / excess_mass, target_prob[:, -1]


def solution(mesh):
    return jax.shard_map(
        verify_local,
        mesh=mesh,
        in_specs=(P(('dp', 'tp'), None, None), P(None, 'tp'), P(('dp', 'tp'), None, None), P('dp', None)),
        out_specs=(P('dp', None), P('dp'), P('dp', None, 'tp'), P('dp', 'tp')),
        check_vma=False,
    )
```

profile of v0, /device:TPU:113, one launch (start us, length us, event | category | flops | bytes accessed | tf_op | source)
XLA Modules:
  0.0 432.1 jit_solution(11039782862175282187)
XLA Ops:
  7.2 0.1 all-gather.2.cloned.1.call-start
  7.2 0.7 all-gather.2.cloned.1.call-update
  8.0 42.4 %copy.14 = f32[32,2,32000]{0,1,2:T(2,128)} copy(f32[32,2,32000]{2,1,0:T(2,128)} %param.6) | data formatting | bytes 16384000 | tf_op args[2]
  50.4 34.6 %reshape.19 = f32[8,1,256000]{2,1,0:T(1,128)} reshape(f32[32000,2,32]{2,1,0:T(2,128)} %bitcast.25) | data formatting | bytes 16384000
  85.0 0.0 copy-start.1
  85.0 6.1 %all-to-all-start = ((f32[8,1,256000]{2,1,0:T(1,128)}), f32[8,1,256000]{2,1,0:T(1,128)}, u32[]{:S(2)}, u32[]{:S(2)}) async-start(f32[8,1,256000]{2,1,0:T(1,128)} %reshape.19), calls=%async_computation | async-start | bytes 16384000 | tf_op jit(solution)/shard_map/all_to_all | solution.py:18
  91.1 0.0 copy-done.1
  91.1 0.1 eq.25
  91.2 91.3 %all-to-all-done = f32[8,1,256000]{2,1,0:T(1,128)} async-done(((f32[8,1,256000]{2,1,0:T(1,128)}), f32[8,1,256000]{2,1,0:T(1,128)}, u32[]{:S(2)}, u32[]{:S(2)}) %all-to-all-start) | async-done | bytes 8192032 | tf_op jit(solution)/shard_map/all_to_all | solution.py:18
  182.5 0.5 broadcast.6
  183.0 25.0 %reduce.1 = f32[8,256000]{1,0:T(8,128)} reduce(f32[8,1,256000]{2,1,0:T(1,128)} %all-to-all-done, f32[]{:T(128)} %broadcast.6), dimensions={1}, to_apply=%all_to_all.13.reduce_sub_computation | reduce | bytes 16384004 | tf_op jit(solution)/shard_map/all_to_all | solution.py:18
  208.0 53.9 %reshape.20 = f32[32000,2,32]{2,1,0:T(2,128)} reshape(f32[8,256000]{1,0:T(8,128)} %reduce.1) | data formatting | bytes 16384000
  262.0 39.9 %copy.15 = f32[32,2,8,4000]{3,0,2,1:T(8,128)} copy(f32[32,2,8,4000]{0,1,3,2:T(2,128)} %bitcast.24) | data formatting | bytes 16384000 | tf_op jit(solution)/shard_map/all_to_all | solution.py:18
  301.9 4.6 %fusion.4 = f32[8,32,2]{1,0,2:T(8,128)S(1)} fusion(f32[32,2,8,4000]{3,0,2,1:T(8,128)} %copy.15, s32[8,32,2]{1,0,2:T(8,128)S(1)} %eq.25), kind=kLoop, calls=%fused_computation.7 | loop fusion | flops 6143488 | bytes 8196096 | tf_op jit(solution)/shard_map/reduce_sum | solution.py:22
  306.5 0.1 stack.10
  306.6 8.8 %copy.16 = f32[256,2,4000]{0,2,1:T(8,128)} copy(f32[256,2,4000]{2,0,1:T(8,128)} %bitcast.26) | data formatting | bytes 16384000 | tf_op jit(solution)/shard_map/all_to_all | solution.py:18
  315.4 0.0 all-gather.2.cloned.1.call-done
  315.4 32.6 %multiply_reduce_fusion = (f32[256,3]{0,1:T(4,128)S(1)}, f32[256,3,4000]{0,2,1:T(8,128)}) fusion(bf16[256,3,4096]{2,0,1:T(8,128)(2,1)} %all-gather.2.cloned.1.call-done, bf16[4096,4000]{0,1:T(8,128)(2,1)} %param.5), kind=kOutput, calls=%fused_computation.3 | convolution fusion | flops 25171968000 | bytes 51350528 | tf_op jit(solution)/shard_map/bgd,dv->bgv/dot_general | solution.py:12
  348.0 12.9 %pmax.7 = f32[256,3]{0,1:T(4,128)S(1)} all-reduce(f32[256,3]{0,1:T(4,128)S(1)} %get-tuple-element.8), channel_id=1, replica_groups=mesh['dp'=2,'tp'=8] {'tp'}, use_global_device_ids=true, to_apply=%region_1.0 | all-reduce | flops 768 | bytes 6144 | tf_op jit(solution)/shard_map/pmax | solution.py:13
  360.9 6.5 %fusion.3 = f32[256,3]{0,1:T(4,128)S(1)} fusion(f32[256,3,4000]{0,2,1:T(8,128)} %get-tuple-element.9, f32[256,3]{0,1:T(4,128)S(1)} %pmax.7), kind=kLoop, calls=%fused_computation.5 | loop fusion | flops 9215232 | bytes 12294144 | tf_op jit(solution)/shard_map/reduce_sum | solution.py:15
  367.4 12.8 %psum.21 = f32[256,3]{0,1:T(4,128)S(1)} all-reduce(f32[256,3]{0,1:T(4,128)S(1)} %fusion.3), channel_id=1, replica_groups=mesh['dp'=2,'tp'=8] {'tp'}, use_global_device_ids=true, to_apply=%region_3.0 | all-reduce | flops 768 | bytes 6144 | tf_op jit(solution)/shard_map/psum | solution.py:15
  380.2 10.9 %fusion.2 = f32[256,3,4000]{0,2,1:T(8,128)} fusion(f32[256,3,4000]{0,2,1:T(8,128)} %get-tuple-element.9, f32[256,3]{0,1:T(4,128)S(1)} %psum.21, f32[256,3]{0,1:T(4,128)S(1)} %pmax.7), kind=kLoop, calls=%fused_computation.4 | loop fusion | flops 9216000 | bytes 24582144 | tf_op jit(solution)/shard_map/div | solution.py:16
  391.1 4.4 %slice_bitcast_fusion = f32[256,4000]{0,1:T(8,128)} fusion(f32[256,3,4000]{0,2,1:T(8,128)} %fusion.2), kind=kLoop, calls=%fused_computation.12 | loop fusion | bytes 8192000 | tf_op jit(solution)/shard_map/squeeze | solution.py:28
  395.5 6.6 %fusion.5 = (f32[256,2]{0,1:T(2,128)S(1)}, f32[256,2]{0,1:T(2,128)S(1)}) fusion(f32[256,2,4000]{0,2,1:T(8,128)} %copy.16, f32[256,3,4000]{0,2,1:T(8,128)} %fusion.2, s32[256,2]{0,1:T(2,128)S(1)} %broadcast_subtract_fusion), kind=kLoop, calls=%fused_computation.14 | loop fusion | flops 12286976 | bytes 16390144 | tf_op jit(solution)/shard_map/reduce_sum | solution.py:27
  402.1 12.7 %all-reduce = (f32[2,256,2]{1,2,0:T(2,128)S(1)}, f32[256,2]{0,1:T(2,128)S(1)}) all-reduce(f32[2,256,2]{1,2,0:T(2,128)S(1)} %pad_maximum_fusion, f32[256,2]{0,1:T(2,128)S(1)} %get-tuple-element.4), channel_id=1, replica_groups=mesh['dp'=2,'tp'=8] {'tp'}, use_global_device_ids=true, to_apply=%region_6.7 | all-reduce | flops 1536 | bytes 12288 | tf_op jit(solution)/shard_map/psum | solution.py:23
  414.8 0.0 copy-start
  414.8 9.6 %broadcast_divide_fusion = f32[256,2,4000]{0,2,1:T(8,128)} fusion(f32[256,2]{0,1:T(2,128)S(1)} %get-tuple-element.7, f32[256,2,4000]{0,2,1:T(8,128)} %copy.16, f32[256,3,4000]{0,2,1:T(8,128)} %fusion.2), kind=kLoop, calls=%fused_computation.13 | loop fusion | flops 6144000 | bytes 24578048 | tf_op jit(solution)/shard_map/div | solution.py:28
  424.5 0.0 copy-done
  424.5 0.6 reduce_sum.48
  (4 shorter events, 0.0 us)
Async XLA Ops:
  7.2 308.3 %all-gather.2.cloned.1.call-start = ((), (), s32[]{:S(2)}) async-start(), calls=%async_computation.1 | async-start | bytes 7077888 | tf_op jit(solution)/shard_map/all_gather | solution.py:11
  85.0 6.2 %copy-start.1 = (s32[256,2]{0,1:T(2,128)S(1)}, s32[256,2]{0,1:T(2,128)}, u32[]{:S(2)}) copy-start(s32[256,2]{0,1:T(2,128)} %param.7) | copy-start | bytes 6148
  85.0 97.5 %all-to-all-start = ((f32[8,1,256000]{2,1,0:T(1,128)}), f32[8,1,256000]{2,1,0:T(1,128)}, u32[]{:S(2)}, u32[]{:S(2)}) async-start(f32[8,1,256000]{2,1,0:T(1,128)} %reshape.19), calls=%async_computation | async-start | bytes 16384000 | tf_op jit(solution)/shard_map/all_to_all | solution.py:18
  414.8 9.6 %copy-start = (f32[256,2]{0,1:T(2,128)}, f32[256,2]{0,1:T(2,128)S(1)}, u32[]{:S(2)}) copy-start(f32[256,2]{0,1:T(2,128)S(1)} %minimum_bitcast_fusion) | copy-start | bytes 6148
Sparse Core Ops, SparseCore 0:
  9.6 39.8 all-gather.1
where the time goes:
time: 440 us; the launch traced here: 432 us
  local copies, waits for them, and re-layouts  185 us (42%)
  waiting for transfers between devices  92 us (21%)
  other arithmetic  63.9 us (15%)
  blocking collectives  38.4 us (9%)
  matrix products  32.6 us (7%)
  between operations  14.3 us (3%)
  starting transfers between devices  6.21 us (1%)
    unnamed x7, local copies, waits for them, and re-layouts  131 us
    all_to_all x1, waiting for transfers between devices, verify_local(): q_cols = lax.all_to_all(q_rows, 'tp', 2, 0, tiled=True)  91.3 us
    all_to_all x3, local copies, waits for them, and re-layouts, verify_local(): q_cols = lax.all_to_all(q_rows, 'tp', 2, 0, tiled=True)  49.3 us
    dot_general x1, matrix products, verify_local(): jnp.einsum('bgd,dv->bgv', hid_all, w_cols, preferred_element_type=jnp.flo...  32.6 us
    all_to_all x1, other arithmetic, verify_local(): q_cols = lax.all_to_all(q_rows, 'tp', 2, 0, tiled=True)  25 us
    pmax x1, blocking collectives, verify_local(): glob_max = lax.pmax(jnp.max(logits, axis=-1, keepdims=True), 'tp')  12.9 us
    psum x1, blocking collectives, verify_local(): exp_total = lax.psum(jnp.sum(exp_terms, axis=-1, keepdims=True), 'tp')  12.8 us
    psum x1, blocking collectives, verify_local(): pick_pair = lax.psum(jnp.stack([p_pick, q_pick]), 'tp')  12.7 us
  transfers between devices with their start and end apart: 2, of which 1 were waited for; matrix products, arithmetic and copies ran while one was open for 49% of the time, Pallas kernels for 0%

commit v1 on v0

v1 whole, which is shorter than its diff:
```python
import functools

import jax
import jax.numpy as jnp
from jax import lax
from jax.experimental import pallas as pl
from jax.experimental.pallas import tpu as pltpu
from jax.experimental.layout import Layout, with_layout_constraint
from jax.sharding import PartitionSpec as P

INV_TEMP = 1.25
TOP = 65535.0
HALF = 32768
LANES = 128
SEGS = 4
STEPS = 10
F32 = jnp.float32
MESH = pl.DeviceIdType.MESH


def kernel(
    n, tok_ref, hid_ref, w_ref, q_ref,
    ex_ref, bonus_ref, small_ref,
    hall, z, stage, scode, qall, rbuf, wbuf, msgs, mass, rowc,
    h_send, h_fwd, h_recv, q_send, q_recv, r_send, r_recv,
    m_send, m_recv, x_send, x_recv, loc, wsem, osem,
):
    k = lax.axis_index("tp")
    x, c = k // 2, k % 2
    chips = n // 2
    right, left = (x + 1) % chips, (x + chips - 1) % chips
    far = (x + 2) % chips
    mate = 2 * x + 1 - c
    positions, batch, dim = hall.shape
    drafts = positions - 1
    rows = batch // n
    vocab = w_ref.shape[0]
    width = qall.shape[2]
    seg = width // SEGS
    tiles = width // LANES
    pitch = q_ref.shape[0] // rows
    all_tiles = pitch // drafts
    off = (k * vocab) % LANES
    hcol = dim // 2
    wrows = vocab // STEPS

    def remote(src, dst, ssem, rsem, who):
        return pltpu.make_async_remote_copy(
            src_ref=src, dst_ref=dst, send_sem=ssem, recv_sem=rsem,
            device_id={"tp": who}, device_id_type=MESH,
        )

    hid_cp = pltpu.make_async_copy(hid_ref, hall.at[:, pl.ds(k * rows, rows), :], loc.at[0])
    hid_cp.start()

    def stage_cp(g):
        part = pl.ds(g * 8 * pitch, 8 * pitch)
        return pltpu.make_async_copy(q_ref.at[part], stage.at[part], loc.at[1 + g])

    for g in range(rows // 8):
        stage_cp(g).start()

    def w_cp(t, slot):
        return pltpu.make_async_copy(
            w_ref.at[pl.ds(pl.multiple_of(t * wrows, 8), wrows)], wbuf.at[slot], wsem.at[slot]
        )

    barrier = pltpu.get_barrier_semaphore()
    for p in range(1, n):
        pl.semaphore_signal(barrier, inc=1, device_id={"tp": (k + p) % n}, device_id_type=MESH)
    pl.semaphore_wait(barrier, n - 1)

    def hpiece(src, half):
        return hall.at[:, pl.ds(pl.multiple_of(src * rows, rows), rows), pl.ds(half * hcol, hcol)]

    def hcopy(src, half, ssem, who):
        return remote(hpiece(src, half), hpiece(src, half), ssem, h_recv.at[src * 2 + half], who)

    def hwait(src, half):
        hcopy(src, half, h_send.at[0], mate).wait_recv()

    hid_cp.wait()
    own_sends = []
    for idx, (who, half) in enumerate(
        [(2 * right + c, 0), (2 * left + c, 1), (2 * right + c, 1), (2 * left + c, 0), (mate, 0), (mate, 1)]
    ):
        cp = hcopy(k, half, h_send.at[idx], who)
        cp.start()
        own_sends.append(cp)
    w_cp(0, 0).start()
    w_cp(1, 1).start()

    z[:, 0:96, :] = jnp.zeros((positions, 96, batch), F32)
    z[:, width - 96:width, :] = jnp.zeros((positions, 96, batch), F32)

    for g in range(rows // 8):
        stage_cp(g).wait()

    def qrows(g, i, j):
        return stage[pl.ds(g * 8 * pitch + drafts * j + i, 8, stride=pitch), :]

    groups = [(i, g) for i in range(drafts) for g in range(rows // 8)]
    lane_b = lax.broadcasted_iota(jnp.int32, (8, batch), 1)
    sub_b = lax.broadcasted_iota(jnp.int32, (8, batch), 0)
    lane_t = lax.broadcasted_iota(jnp.int32, (8, LANES), 1)
    mine = [lane_b == k * rows + 8 * g + sub_b for g in range(rows // 8)]
    tok_col = []
    for i, g in groups:
        t = jnp.where(mine[g], jnp.broadcast_to(tok_ref[i:i + 1, :].astype(F32), (8, batch)), 0.0)
        tok_col.append(jnp.broadcast_to(jnp.sum(t, axis=1, keepdims=True), (8, LANES)).astype(jnp.int32))

    def scan(j, carry):
        top, got = carry
        new_top, new_got = [], []
        col = lane_t + j * LANES
        for a, (i, g) in enumerate(groups):
            v = qrows(g, i, j)
            new_top.append(jnp.maximum(top[a], v))
            new_got.append(jnp.where(col == tok_col[a], v, got[a]))
        return tuple(new_top), tuple(new_got)

    zero8 = tuple(jnp.zeros((8, LANES), F32) for _ in groups)
    top, got = lax.fori_loop(0, all_tiles, scan, (zero8, zero8))
    qtop_row, qgot_row = [], []
    for i in range(drafts):
        acc_t = jnp.zeros((8, batch), F32)
        acc_g = jnp.zeros((8, batch), F32)
        for a, (ii, g) in enumerate(groups):
            if ii != i:
                continue
            tcol = jnp.max(top[a], axis=1, keepdims=True)
            gcol = jnp.sum(got[a], axis=1, keepdims=True)
            rowc[a] = jnp.broadcast_to(jnp.log(TOP) - 0.25 * jnp.log(tcol), (8, LANES))
            acc_t = acc_t + jnp.where(mine[g], jnp.broadcast_to(tcol, (8, batch)), 0.0)
            acc_g = acc_g + jnp.where(mine[g], jnp.broadcast_to(gcol, (8, batch)), 0.0)
        qtop_row.append(jnp.sum(acc_t, axis=0, keepdims=True))
        qgot_row.append(jnp.sum(acc_g, axis=0, keepdims=True))
    msgs[k] = jnp.zeros(msgs.shape[1:], F32)
    for i in range(drafts):
        msgs[k, 8 + i:9 + i, :] = qgot_row[i]
        msgs[k, 10 + i:11 + i, :] = qtop_row[i]

    def encode(dest, put):
        first = (dest * vocab) // LANES

        def body(j, _):
            for i in range(drafts):
                for gg in range(rows // 16):
                    parts = []
                    for g in (2 * gg, 2 * gg + 1):
                        v = qrows(g, i, first + j)
                        y = jnp.exp(0.25 * jnp.log(v) + rowc[i * (rows // 8) + g])
                        parts.append((y + 0.5).astype(jnp.int32) - HALF)
                    code = jnp.concatenate(parts, axis=0).astype(jnp.int16)
                    put(i, gg, pl.ds(pl.multiple_of(j * LANES, LANES), LANES), code)
            return 0

        lax.fori_loop(0, tiles, body, 0)

    def to_slot(r):
        def put(i, gg, cols, code):
            scode[r, i, 16 * gg:16 * gg + 16, cols] = code

        return put

    def to_self(i, gg, cols, code):
        qall[i, pl.ds(pl.multiple_of(k * rows + 16 * gg, 16), 16), cols] = code

    encode(2 * far, to_slot(0))
    encode(2 * far + 1, to_slot(1))

    fwd = []

    def forward(src, half):
        cp = hcopy(src, half, h_fwd.at[len(fwd)], mate)
        cp.start()
        fwd.append(cp)

    hwait(2 * left + c, 0)
    rel_r = hcopy(2 * left + c, 0, h_send.at[6], 2 * right + c)
    rel_r.start()
    forward(2 * left + c, 0)
    hwait(2 * right + c, 1)
    rel_l = hcopy(2 * right + c, 1, h_send.at[7], 2 * left + c)
    rel_l.start()
    forward(2 * right + c, 1)

    def unit(buf_i, i, s):
        return buf_i.at[i, :, pl.ds(pl.multiple_of(s * seg, LANES), seg)]

    def landing(src, i, s):
        return qall.at[
            i, pl.ds(pl.multiple_of(src * rows, rows), rows), pl.ds(pl.multiple_of(s * seg, LANES), seg)
        ]

    def direct(slot, i, s, who):
        return remote(
            unit(scode.at[slot], i, s), landing(k, i, s),
            q_send.at[slot * 8 + i * SEGS + s], q_recv.at[k * 8 + i * SEGS + s], who,
        )

    def out_far(way, v):
        i, s, cc = v // 4, 2 * ((v // 2) % 2) + way, v % 2
        who = 2 * (right if way == 0 else left) + c
        return remote(
            unit(scode.at[cc], i, s), rbuf.at[way, v],
            q_send.at[cc * 8 + i * SEGS + s], r_recv.at[way * 8 + v], who,
        )

    def relay(way, v):
        i, s, cc = v // 4, 2 * ((v // 2) % 2) + way, v % 2
        src = 2 * (left if way == 0 else right) + c
        who = 2 * (right if way == 0 else left) + cc
        return remote(
            rbuf.at[way, v], landing(src, i, s),
            r_send.at[way * 8 + v], q_recv.at[src * 8 + i * SEGS + s], who,
        )

    def near(way, u):
        i, s, cc = u // 8, (u // 2) % SEGS, u % 2
        who = 2 * (right if way == 0 else left) + cc
        return direct(2 + 2 * way + cc, i, s, who)

    def send_far(v):
        out_far(0, v).start()
        out_far(1, v).start()

    def send_near(u):
        near(0, u).start()
        near(1, u).start()

    def pass_on(v):
        for way in range(2):
            out_far(way, v).wait_recv()
            relay(way, v).start()

    encode(2 * right, to_slot(2))
    encode(2 * right + 1, to_slot(3))
    encode(2 * left, to_slot(4))
    encode(2 * left + 1, to_slot(5))

    hwait(2 * left + c, 1)
    forward(2 * left + c, 1)
    hwait(2 * right + c, 0)
    forward(2 * right + c, 0)

    def first_far(v, _):
        send_far(v)
        return 0

    def first_near(u, _):
        send_near(u)
        return 0

    lax.fori_loop(0, 4, first_far, 0)
    lax.fori_loop(0, 8, first_near, 0)
    encode(mate, to_slot(6))
    encode(k, to_self)

    def to_mate(u, _):
        direct(6, u // SEGS, u % SEGS, mate).start()
        return 0

    lax.fori_loop(0, drafts * SEGS, to_mate, 0)

    hwait(2 * far + c, 0)
    forward(2 * far + c, 0)
    hwait(2 * far + c, 1)
    forward(2 * far + c, 1)
    for chip in (x, left, right, far):
        for half in range(2):
            hwait(2 * chip + 1 - c, half)

    def step(t, top):
        slot = t % 2

        @pl.when((t >= 2) & (t < 4))
        def _():
            pass_on(2 * (t - 2))
            pass_on(2 * (t - 2) + 1)

        @pl.when((t >= 4) & (t < 6))
        def _():
            send_far(4 + 2 * (t - 4))
            send_far(4 + 2 * (t - 4) + 1)

        @pl.when(t >= 8)
        def _():
            send_near(8 + 2 * (t - 8))
            send_near(8 + 2 * (t - 8) + 1)

        w_cp(t, slot).wait()
        prod = INV_TEMP * lax.dot_general(
            wbuf[slot], hall[...].reshape(positions * batch, dim), (((1,), (1,)), ((), ())), preferred_element_type=F32
        )
        base = pl.multiple_of(off + t * wrows, 8)
        for i in range(positions):
            z[i, pl.ds(base, wrows), :] = prod[:, i * batch:(i + 1) * batch]

        @pl.when(t + 2 < STEPS)
        def _():
            w_cp(t + 2, slot).start()

        return jnp.maximum(top, jnp.max(prod.reshape(wrows // 8, 8, positions * batch), axis=0))

    top = lax.fori_loop(0, STEPS, step, jnp.full((8, positions * batch), -jnp.inf, F32))
    own_max = jnp.max(top, axis=0, keepdims=True)

    chunk = 160
    row_i = lax.broadcasted_iota(jnp.int32, (chunk, batch), 0)
    for i in range(positions):
        m_i = own_max[:, i * batch:(i + 1) * batch]
        want = tok_ref[i:i + 1, :] - k * vocab if i < drafts else None

        def expo(t, carry, i=i, m_i=m_i, want=want):
            total, got = carry
            at = pl.ds(pl.multiple_of(off + t * chunk, 8), chunk)
            e = jnp.exp(z[i, at, :] - m_i)
            z[i, at, :] = e
            total = total + jnp.sum(e.reshape(chunk // 8, 8, batch), axis=0)
            if want is not None:
                pick = jnp.where(row_i + t * chunk == want, e, 0.0)
                got = got + jnp.sum(pick.reshape(chunk // 8, 8, batch), axis=0)
            return total, got

        zero = jnp.zeros((8, batch), F32)
        total, got = lax.fori_loop(0, vocab // chunk, expo, (zero, zero))
        msgs[k, i:i + 1, :] = m_i
        msgs[k, 3 + i:4 + i, :] = jnp.sum(total, axis=0, keepdims=True)
        if i < drafts:
            msgs[k, 6 + i:7 + i, :] = jnp.sum(got, axis=0, keepdims=True)

    def msg(p, src):
        return remote(msgs.at[src], msgs.at[src], m_send.at[p], m_recv.at[src], (k + p) % n)

    for p in range(1, n):
        msg(p, k).start()

    def rest_near(u, _):
        send_near(u)
        return 0

    lax.fori_loop(12, 16, rest_near, 0)
    for v in range(4, 8):
        pass_on(v)
    for p in range(1, n):
        msg(p, (k + p) % n).wait_recv()

    allm = msgs[...]
    peak = jnp.max(allm[:, 0:3, :], axis=0)
    part = jnp.exp(allm[:, 0:3, :] - peak[None])
    inv = 1.0 / jnp.sum(part * allm[:, 3:6, :], axis=0)
    p_pick = jnp.sum(part[:, 0:drafts, :] * allm[:, 6:8, :], axis=0) * inv[0:drafts]
    q_pick = jnp.sum(allm[:, 8:10, :], axis=0)
    q_scale = jnp.sum(allm[:, 10:12, :], axis=0) * (1.0 / (TOP * TOP * TOP * TOP))
    fac = jnp.exp(msgs[k, 0:3, :] - peak) * inv

    def scale(t, _):
        at = pl.ds(pl.multiple_of(off + t * chunk, 8), chunk)
        z[drafts, at, :] = z[drafts, at, :] * fac[drafts:drafts + 1, :]
        return 0

    lax.fori_loop(0, vocab // chunk, scale, 0)

    def out_cp(i, dst):
        return pltpu.make_async_copy(z.at[i, pl.ds(pl.multiple_of(off, 8), vocab), :], dst, osem.at[i])

    out_cp(drafts, bonus_ref).start()

    def xmsg(p, i, src):
        return remote(mass.at[i, src], mass.at[i, src], x_send.at[i * n + p], x_recv.at[i * n + src], (k + p) % n)

    for i in range(drafts):
        acc = [jnp.zeros((8, LANES), F32) for _ in range(batch // LANES)]
        for s in range(SEGS):
            for p in range(1, n):
                src = (k + p) % n
                remote(
                    landing(src, i, s), landing(src, i, s), q_send.at[0],
                    q_recv.at[src * 8 + i * SEGS + s], mate,
                ).wait_recv()

            def body(t, acc, i=i, s=s):
                at = pl.ds(pl.multiple_of((s * (tiles // SEGS) + t) * LANES, LANES), LANES)
                out = []
                for h in range(batch // LANES):
                    ls = slice(h * LANES, (h + 1) * LANES)
                    code = qall[i, ls, at].astype(jnp.int32).astype(F32)
                    y = code.T + float(HALF)
                    y = y * y
                    qt = y * y * q_scale[i:i + 1, ls]
                    ex = jnp.maximum(z[i, at, ls] * fac[i:i + 1, ls] - qt, 0.0)
                    z[i, at, ls] = ex
                    out.append(acc[h] + jnp.sum(ex.reshape(LANES // 8, 8, LANES), axis=0))
                return tuple(out)

            acc = lax.fori_loop(0, tiles // SEGS, body, tuple(acc))
        out_cp(i, ex_ref.at[i]).start()
        for h in range(batch // LANES):
            mass[i, k, :, h * LANES:(h + 1) * LANES] = acc[h]
        for p in range(1, n):
            xmsg(p, i, k).start()
    small_ref[...] = jnp.zeros(small_ref.shape, F32)
    small_ref[2:4, :] = p_pick
    small_ref[4:6, :] = q_pick
    for i in range(drafts):
        for p in range(1, n):
            xmsg(p, i, (k + p) % n).wait_recv()
        total = jnp.sum(jnp.sum(mass[i], axis=0), axis=0, keepdims=True)
        small_ref[i:i + 1, :] = 1.0 / total

    for cp in own_sends + [rel_r, rel_l] + fwd:
        cp.wait_send()
    for p in range(1, n):
        msg(p, k).wait_send()
        for i in range(drafts):
            xmsg(p, i, k).wait_send()

    def drain(u, _):
        direct(u // 8, (u % 8) // SEGS, u % SEGS, mate).wait_send()
        return 0

    lax.fori_loop(0, 7 * 8, drain, 0)

    def drain_relay(v, _):
        relay(0, v).wait_send()
        relay(1, v).wait_send()
        return 0

    lax.fori_loop(0, 8, drain_relay, 0)
    out_cp(drafts, bonus_ref).wait()
    for i in range(drafts):
        out_cp(i, ex_ref.at[i]).wait()


def solution(mesh):
    n = mesh.shape["tp"]

    def local(hid, w, q, tok):
        rows, positions, dim = hid.shape
        vocab = w.shape[1]
        drafts = positions - 1
        batch = rows * n
        q_tiles = q.shape[2] // LANES
        width = -(-vocab // LANES) * LANES
        q_view = q.reshape(rows, drafts, q_tiles, LANES).transpose(0, 2, 1, 3)
        q_view = with_layout_constraint(q_view, Layout((0, 1, 2, 3))).reshape(-1, LANES)
        dma = pltpu.SemaphoreType.DMA
        ex, bonus, small = pl.pallas_call(
            functools.partial(kernel, n),
            out_shape=(
                jax.ShapeDtypeStruct((drafts, vocab, batch), F32),
                jax.ShapeDtypeStruct((vocab, batch), F32),
                jax.ShapeDtypeStruct((8, batch), F32),
            ),
            in_specs=[pl.BlockSpec(memory_space=pltpu.VMEM)] + [pl.BlockSpec(memory_space=pl.ANY)] * 3,
            out_specs=(
                pl.BlockSpec(memory_space=pl.ANY),
                pl.BlockSpec(memory_space=pl.ANY),
                pl.BlockSpec(memory_space=pltpu.VMEM),
            ),
            scratch_shapes=[
                pltpu.VMEM((positions, batch, dim), jnp.bfloat16),
                pltpu.VMEM((positions, width, batch), F32),
                pltpu.VMEM((rows * q_tiles * drafts, LANES), F32),
                pltpu.VMEM((n - 1, drafts, rows, width), jnp.int16),
                pltpu.VMEM((drafts, batch, width), jnp.int16),
                pltpu.VMEM((2, 8, rows, width // SEGS), jnp.int16),
                pltpu.VMEM((2, vocab // STEPS, dim), jnp.bfloat16),
                pltpu.VMEM((n, 16, batch), F32),
                pltpu.VMEM((drafts, n, 8, batch), F32),
                pltpu.VMEM((drafts * (rows // 8), 8, LANES), F32),
                dma((8,)), dma((8,)), dma((2 * n,)),
                dma((7 * 8,)), dma((8 * 8,)), dma((16,)), dma((16,)),
                dma((n,)), dma((n,)), dma((2 * n,)), dma((2 * n,)),
                dma((8,)), dma((2,)), dma((3,)),
            ],
            compiler_params=pltpu.CompilerParams(
                collective_id=0, has_side_effects=True, vmem_limit_bytes=60 * 2**20
            ),
        )(tok.T, hid.transpose(1, 0, 2), w.T, q_view)
        residual = (ex * small[0:drafts][:, None, :]).transpose(2, 0, 1)
        accept = jnp.minimum(small[2:4] / small[4:6], 1.0)
        expected = accept[0] + accept[0] * accept[1]
        return accept.T, expected, residual, bonus.T

    return jax.shard_map(
        local,
        mesh=mesh,
        in_specs=(P(("dp", "tp"), None, None), P(None, "tp"), P(("dp", "tp"), None, None), P("dp", None)),
        out_specs=(P("dp", None), P("dp"), P("dp", None, "tp"), P("dp", "tp")),
        check_vma=False,
    )
```

time: 440 us -> 102 us (0.23); the launches traced: 432 us -> 101 us
  local copies, waits for them, and re-layouts: 185 us -> 1.99 us
  waiting for transfers between devices: 92 us -> 0 us
  Pallas kernels: 0 us -> 90 us
  other arithmetic: 63.9 us -> 8.75 us
  blocking collectives: 38.4 us -> 0 us
  matrix products: 32.6 us -> 0 us
  between operations: 14.3 us -> 0.66 us
  starting transfers between devices: 6.21 us -> 0 us
    unnamed x7 -> x5, local copies, waits for them, and re-layouts: 131 us -> 1.98 us
    all_to_all x1 -> x0, waiting for transfers between devices: 91.3 us -> none  [verify_local(): q_cols = lax.all_to_all(q_rows, 'tp', 2, 0, tiled=True)]
    pallas_call x0 -> x1, Pallas kernels: none -> 90 us  [local(): pl.pallas_call(functools.partial(kernel, n), out_shape=(jax.ShapeDtypeStr...]
    all_to_all x3 -> x0, local copies, waits for them, and re-layouts: 49.3 us -> none  [verify_local(): q_cols = lax.all_to_all(q_rows, 'tp', 2, 0, tiled=True)]
    dot_general x1 -> x0, matrix products: 32.6 us -> none  [verify_local(): jnp.einsum('bgd,dv->bgv', hid_all, w_cols, preferred_element_type=jnp.flo...]
    psum x2 -> x0, blocking collectives: 25.5 us -> none  [the longest x1 12.8 us: verify_local(): exp_total = lax.psum(jnp.sum(exp_terms, axis=-1, keepdims=True), 'tp')]
    all_to_all x1 -> x0, other arithmetic: 25 us -> none  [verify_local(): q_cols = lax.all_to_all(q_rows, 'tp', 2, 0, tiled=True)]
    div x2 -> x0, other arithmetic: 20.5 us -> none  [the longest x1 10.9 us: verify_local(): target_prob = exp_terms / exp_total]
  transfers between devices with their start and end apart: 2 -> 0, of which waited for: 1 -> 0; matrix products, arithmetic and copies ran while one was open for 49% -> 0% of each run, Pallas kernels for 0% -> 0%
where the time goes in v1:
time: 102 us; the launch traced here: 101 us
  Pallas kernels  90 us (88%)
  other arithmetic  8.75 us (9%)
  local copies, waits for them, and re-layouts  1.99 us (2%)
    pallas_call x1, Pallas kernels, local(): pl.pallas_call(functools.partial(kernel, n), out_shape=(jax.ShapeDtypeStr...  90 us
    transpose x1, other arithmetic, local(): residual = (ex * small[0:drafts][:, None, :]).transpose(2, 0, 1)  7.37 us

profile of v1, /device:TPU:113, one launch (start us, length us, event | category | flops | bytes accessed | tf_op | source)
XLA Modules:
  0.0 101.4 jit_solution(17711355383336952678)
XLA Ops:
  0.6 90.0 %shard_map.75 = (f32[2,4000,256]{2,1,0:T(8,128)}, f32[4000,256]{1,0:T(8,128)}, f32[8,256]{1,0:T(8,128)}) custom-call(s32[2,256]{1,0:T(2,128)} %bitcast.21, bf16[3,32,4096]{2,1,0:T(8,128)(2,1)} %bitcast.17, bf16[4000,4096]{1,0:T(8,128)(2,1)} %bitcast.14, f32[16000,128]{1,0:T(8,128)} %bitcast.15), custom_call_target="tpu_custom_call" | custom-call | tf_op jit(solution)/shard_map/pallas_call | solution.py:449
  90.7 0.8 fusion.1
  91.5 0.0 copy-start.1
  91.5 0.0 copy-start
  91.5 7.4 %multiply_bitcast_fusion = f32[256,2,4000]{0,2,1:T(8,128)} fusion(f32[2,4000,256]{2,1,0:T(8,128)} %get-tuple-element.8, f32[2,256]{1,0:T(2,128)S(1)} %get-tuple-element.10), kind=kLoop, calls=%fused_computation | loop fusion | flops 2048000 | bytes 16386048 | tf_op jit(solution)/shard_map/transpose | solution.py:482
  98.9 0.0 copy-done.1
  98.9 0.6 multiply_add_fusion
  99.4 0.0 copy-done
  99.4 2.0 %copy.9 = f32[256,4000]{0,1:T(8,128)} copy(f32[256,4000]{0,1:T(8,128)S(1)} %bitcast.16) | data formatting | bytes 8192000
  (1 shorter events, 0.0 us)
Async XLA Ops:
  91.5 7.4 %copy-start.1 = (f32[2,256]{1,0:T(2,128)}, f32[2,256]{1,0:T(2,128)S(1)}, u32[]{:S(2)}) copy-start(f32[2,256]{1,0:T(2,128)S(1)} %get-tuple-element.11) | copy-start | bytes 6148
  91.5 8.0 %copy-start = (f32[4000,256]{1,0:T(8,128)S(1)}, f32[4000,256]{1,0:T(8,128)}, u32[]{:S(2)}) copy-start(f32[4000,256]{1,0:T(8,128)} %get-tuple-element.9) | copy-start | bytes 12288004

commit v2 on v1

--- a/solution.py
+++ b/solution.py
@@ -14,16 +14,17 @@
 LANES = 128
 SEGS = 4
 STEPS = 10
+PARTS = 5
 F32 = jnp.float32
 MESH = pl.DeviceIdType.MESH
 
 
 def kernel(
-    n, tok_ref, hid_ref, w_ref, q_ref,
-    ex_ref, bonus_ref, small_ref,
-    hall, z, stage, scode, qall, rbuf, wbuf, msgs, mass, rowc,
+    n, tok_in, hid_ref, w_ref, q_ref,
+    z, small_ref,
+    tok_ref, hall, stage, scode, qall, rbuf, wbuf, msgs, mass, rowc,
     h_send, h_fwd, h_recv, q_send, q_recv, r_send, r_recv,
-    m_send, m_recv, x_send, x_recv, loc, wsem, osem,
+    m_send, m_recv, x_send, x_recv, loc, wsem,
 ):
     k = lax.axis_index("tp")
     x, c = k // 2, k % 2
@@ -52,6 +53,8 @@
 
     hid_cp = pltpu.make_async_copy(hid_ref, hall.at[:, pl.ds(k * rows, rows), :], loc.at[0])
     hid_cp.start()
+    tok_cp = pltpu.make_async_copy(tok_in, tok_ref, loc.at[6])
+    tok_cp.start()
 
     def stage_cp(g):
         part = pl.ds(g * 8 * pitch, 8 * pitch)
@@ -93,6 +96,7 @@
     z[:, 0:96, :] = jnp.zeros((positions, 96, batch), F32)
     z[:, width - 96:width, :] = jnp.zeros((positions, 96, batch), F32)
 
+    tok_cp.wait()
     for g in range(rows // 8):
         stage_cp(g).wait()
 
@@ -362,11 +366,6 @@
 
     lax.fori_loop(0, vocab // chunk, scale, 0)
 
-    def out_cp(i, dst):
-        return pltpu.make_async_copy(z.at[i, pl.ds(pl.multiple_of(off, 8), vocab), :], dst, osem.at[i])
-
-    out_cp(drafts, bonus_ref).start()
-
     def xmsg(p, i, src):
         return remote(mass.at[i, src], mass.at[i, src], x_send.at[i * n + p], x_recv.at[i * n + src], (k + p) % n)
 
@@ -395,7 +394,6 @@
                 return tuple(out)
 
             acc = lax.fori_loop(0, tiles // SEGS, body, tuple(acc))
-        out_cp(i, ex_ref.at[i]).start()
         for h in range(batch // LANES):
             mass[i, k, :, h * LANES:(h + 1) * LANES] = acc[h]
         for p in range(1, n):
@@ -428,9 +426,28 @@
         return 0
 
     lax.fori_loop(0, 8, drain_relay, 0)
-    out_cp(drafts, bonus_ref).wait()
+
+
+def finish(n, z, small, res_ref, bonus_ref, acc_ref, exp_ref, buf, sem):
+    drafts, vocab, _ = res_ref.shape
+    off = pl.multiple_of((lax.axis_index("tp") * vocab) % LANES, 8)
+    last = pltpu.make_async_copy(z.at[drafts, pl.ds(off, vocab), :], bonus_ref, sem.at[0])
+    last.start()
+    copies = [last]
+    part = vocab // PARTS
     for i in range(drafts):
-        out_cp(i, ex_ref.at[i]).wait()
+        scale = small[i:i + 1, :]
+        for t in range(PARTS):
+            to = pl.ds(t * part, part)
+            buf[i, to, :] = z[i, pl.ds(pl.multiple_of(off + t * part, 8), part), :] * scale
+            cp = pltpu.make_async_copy(buf.at[i, to], res_ref.at[i, to], sem.at[len(copies)])
+            cp.start()
+            copies.append(cp)
+    accept = jnp.minimum(small[2:4, :] / small[4:6, :], 1.0)
+    acc_ref[...] = accept
+    exp_ref[...] = accept[0:1] + accept[0:1] * accept[1:2]
+    for cp in copies:
+        cp.wait()
 
 
 def solution(mesh):
@@ -446,22 +463,18 @@
         q_view = q.reshape(rows, drafts, q_tiles, LANES).transpose(0, 2, 1, 3)
         q_view = with_layout_constraint(q_view, Layout((0, 1, 2, 3))).reshape(-1, LANES)
         dma = pltpu.SemaphoreType.DMA
-        ex, bonus, small = pl.pallas_call(
+        vmem, anywhere = pl.BlockSpec(memory_space=pltpu.VMEM), pl.BlockSpec(memory_space=pltpu.HBM)
+        z, small = pl.pallas_call(
             functools.partial(kernel, n),
             out_shape=(
-                jax.ShapeDtypeStruct((drafts, vocab, batch), F32),
-                jax.ShapeDtypeStruct((vocab, batch), F32),
+                jax.ShapeDtypeStruct((positions, width, batch), F32),
                 jax.ShapeDtypeStruct((8, batch), F32),
             ),
-            in_specs=[pl.BlockSpec(memory_space=pltpu.VMEM)] + [pl.BlockSpec(memory_space=pl.ANY)] * 3,
-            out_specs=(
-                pl.BlockSpec(memory_space=pl.ANY),
-                pl.BlockSpec(memory_space=pl.ANY),
-                pl.BlockSpec(memory_space=pltpu.VMEM),
-            ),
+            in_specs=[anywhere] * 4,
+            out_specs=(vmem, vmem),
             scratch_shapes=[
+                pltpu.VMEM((drafts, batch), jnp.int32),
                 pltpu.VMEM((positions, batch, dim), jnp.bfloat16),
-                pltpu.VMEM((positions, width, batch), F32),
                 pltpu.VMEM((rows * q_tiles * drafts, LANES), F32),
                 pltpu.VMEM((n - 1, drafts, rows, width), jnp.int16),
                 pltpu.VMEM((drafts, batch, width), jnp.int16),
@@ -473,16 +486,26 @@
                 dma((8,)), dma((8,)), dma((2 * n,)),
                 dma((7 * 8,)), dma((8 * 8,)), dma((16,)), dma((16,)),
                 dma((n,)), dma((n,)), dma((2 * n,)), dma((2 * n,)),
-                dma((8,)), dma((2,)), dma((3,)),
+                dma((8,)), dma((2,)),
             ],
             compiler_params=pltpu.CompilerParams(
-                collective_id=0, has_side_effects=True, vmem_limit_bytes=60 * 2**20
+                collective_id=0, has_side_effects=True, vmem_limit_bytes=40 * 2**20
             ),
-        )(tok.T, hid.transpose(1, 0, 2), w.T, q_view)
-        residual = (ex * small[0:drafts][:, None, :]).transpose(2, 0, 1)
-        accept = jnp.minimum(small[2:4] / small[4:6], 1.0)
-        expected = accept[0] + accept[0] * accept[1]
-        return accept.T, expected, residual, bonus.T
+        )(*[pltpu.with_memory_space_constraint(a, pltpu.HBM) for a in (tok.T, hid.transpose(1, 0, 2), w.T, q_view)])
+        residual, bonus, accept, expected = pl.pallas_call(
+            functools.partial(finish, n),
+            out_shape=(
+                jax.ShapeDtypeStruct((drafts, vocab, batch), F32),
+                jax.ShapeDtypeStruct((vocab, batch), F32),
+                jax.ShapeDtypeStruct((drafts, batch), F32),
+                jax.ShapeDtypeStruct((1, batch), F32),
+            ),
+            in_specs=[vmem, vmem],
+            out_specs=(anywhere, anywhere, vmem, vmem),
+            scratch_shapes=[pltpu.VMEM((drafts, vocab, batch), F32), dma((drafts * PARTS + 1,))],
+            compiler_params=pltpu.CompilerParams(vmem_limit_bytes=24 * 2**20),
+        )(z, small)
+        return accept.T, expected[0], residual.transpose(2, 0, 1), bonus.T
 
     return jax.shard_map(
         local,

time: 102 us -> 94.7 us (0.928)
  other arithmetic: 8.75 us -> 0 us
  Pallas kernels: 90 us -> 94 us
  local copies, waits for them, and re-layouts: 1.99 us -> 0 us
    transpose x1 -> x0, other arithmetic: 7.37 us -> none  [local(): residual = (ex * small[0:drafts][:, None, :]).transpose(2, 0, 1)]
    pallas_call x0 -> x1, Pallas kernels: none -> 5.17 us  [local(): pl.pallas_call(functools.partial(finish, n), out_shape=(jax.ShapeDtypeStr...]
    unnamed x5 -> x0, local copies, waits for them, and re-layouts: 1.98 us -> none
    pallas_call x1, Pallas kernels: 90 us -> 88.8 us  [local(): pl.pallas_call(functools.partial(kernel, n), out_shape=(jax.ShapeDtypeStr...]
where the time goes in v2:
time: 94.7 us
  Pallas kernels  94 us (99%)
    pallas_call x1, Pallas kernels, local(): pl.pallas_call(functools.partial(kernel, n), out_shape=(jax.ShapeDtypeStr...  88.8 us
    pallas_call x1, Pallas kernels, local(): pl.pallas_call(functools.partial(finish, n), out_shape=(jax.ShapeDtypeStr...  5.17 us

profile of v2, /device:TPU:113, one launch (start us, length us, event | category | flops | bytes accessed | tf_op | source)
XLA Modules:
  0.0 94.7 jit_solution(12132427418951608861)
XLA Ops:
  0.6 88.8 %shard_map.75 = (f32[3,4096,256]{2,1,0:T(8,128)S(1)}, f32[8,256]{1,0:T(8,128)S(1)}) custom-call(s32[2,256]{1,0:T(2,128)} %bitcast.15, bf16[3,32,4096]{2,1,0:T(8,128)(2,1)} %bitcast.14, bf16[4000,4096]{1,0:T(8,128)(2,1)} %bitcast.12, f32[16000,128]{1,0:T(8,128)} %bitcast.13), custom_call_target="tpu_custom_call" | custom-call | tf_op jit(solution)/shard_map/pallas_call | solution.py:467
  89.5 5.2 %shard_map.76 = (f32[2,4000,256]{2,1,0:T(8,128)}, f32[4000,256]{1,0:T(8,128)}, f32[2,256]{1,0:T(2,128)}, f32[1,256]{1,0:T(1,128)}) custom-call(f32[3,4096,256]{2,1,0:T(8,128)S(1)} %get-tuple-element.10.z, f32[8,256]{1,0:T(8,128)S(1)} %get-tuple-element.11.small), custom_call_target="tpu_custom_call" | custom-call | tf_op jit(solution)/shard_map/pallas_call | solution.py:495

commit v3 on v2

--- a/solution.py
+++ b/solution.py
@@ -288,10 +288,10 @@
             send_far(4 + 2 * (t - 4))
             send_far(4 + 2 * (t - 4) + 1)
 
-        @pl.when(t >= 8)
+        @pl.when(t >= 6)
         def _():
-            send_near(8 + 2 * (t - 8))
-            send_near(8 + 2 * (t - 8) + 1)
+            send_near(8 + 2 * (t - 6))
+            send_near(8 + 2 * (t - 6) + 1)
 
         w_cp(t, slot).wait()
         prod = INV_TEMP * lax.dot_general(
@@ -340,11 +340,6 @@
     for p in range(1, n):
         msg(p, k).start()
 
-    def rest_near(u, _):
-        send_near(u)
-        return 0
-
-    lax.fori_loop(12, 16, rest_near, 0)
     for v in range(4, 8):
         pass_on(v)
     for p in range(1, n):

time: 94.7 us -> 94.2 us (level)
  no operation moved by 1% of the time
where the time goes in v3:
time: 94.2 us; the launch traced here: 94.1 us
  Pallas kernels  93.5 us (99%)
    pallas_call x1, Pallas kernels, local(): pl.pallas_call(functools.partial(kernel, n), out_shape=(jax.ShapeDtypeStr...  88.3 us
    pallas_call x1, Pallas kernels, local(): pl.pallas_call(functools.partial(finish, n), out_shape=(jax.ShapeDtypeStr...  5.17 us

profile of v3, /device:TPU:113, one launch (start us, length us, event | category | flops | bytes accessed | tf_op | source)
XLA Modules:
  0.0 94.1 jit_solution(6854808600922198253)
XLA Ops:
  0.6 88.3 %shard_map.75 = (f32[3,4096,256]{2,1,0:T(8,128)S(1)}, f32[8,256]{1,0:T(8,128)S(1)}) custom-call(s32[2,256]{1,0:T(2,128)} %bitcast.15, bf16[3,32,4096]{2,1,0:T(8,128)(2,1)} %bitcast.14, bf16[4000,4096]{1,0:T(8,128)(2,1)} %bitcast.12, f32[16000,128]{1,0:T(8,128)} %bitcast.13), custom_call_target="tpu_custom_call" | custom-call | tf_op jit(solution)/shard_map/pallas_call | solution.py:462
  88.9 5.2 %shard_map.76 = (f32[2,4000,256]{2,1,0:T(8,128)}, f32[4000,256]{1,0:T(8,128)}, f32[2,256]{1,0:T(2,128)}, f32[1,256]{1,0:T(1,128)}) custom-call(f32[3,4096,256]{2,1,0:T(8,128)S(1)} %get-tuple-element.10.z, f32[8,256]{1,0:T(8,128)S(1)} %get-tuple-element.11.small), custom_call_target="tpu_custom_call" | custom-call | tf_op jit(solution)/shard_map/pallas_call | solution.py:490

commit v4 on v3

--- a/solution.py
+++ b/solution.py
@@ -293,6 +293,11 @@
             send_near(8 + 2 * (t - 6))
             send_near(8 + 2 * (t - 6) + 1)
 
+        @pl.when(t >= STEPS - 2)
+        def _():
+            pass_on(4 + 2 * (t - (STEPS - 2)))
+            pass_on(4 + 2 * (t - (STEPS - 2)) + 1)
+
         w_cp(t, slot).wait()
         prod = INV_TEMP * lax.dot_general(
             wbuf[slot], hall[...].reshape(positions * batch, dim), (((1,), (1,)), ((), ())), preferred_element_type=F32
@@ -340,8 +345,6 @@
     for p in range(1, n):
         msg(p, k).start()
 
-    for v in range(4, 8):
-        pass_on(v)
     for p in range(1, n):
         msg(p, (k + p) % n).wait_recv()
 

time: 94.2 us -> 99.5 us (1.056)
  Pallas kernels: 93.5 us -> 98.8 us
    pallas_call x1, Pallas kernels: 88.3 us -> 93.6 us  [local(): pl.pallas_call(functools.partial(kernel, n), out_shape=(jax.ShapeDtypeStr...]
where the time goes in v4:
time: 99.5 us; the launch traced here: 99.4 us
  Pallas kernels  98.8 us (99%)
    pallas_call x1, Pallas kernels, local(): pl.pallas_call(functools.partial(kernel, n), out_shape=(jax.ShapeDtypeStr...  93.6 us
    pallas_call x1, Pallas kernels, local(): pl.pallas_call(functools.partial(finish, n), out_shape=(jax.ShapeDtypeStr...  5.17 us

profile of v4, /device:TPU:113, one launch (start us, length us, event | category | flops | bytes accessed | tf_op | source)
XLA Modules:
  0.0 99.4 jit_solution(17455775121009228703)
XLA Ops:
  0.6 93.6 %shard_map.75 = (f32[3,4096,256]{2,1,0:T(8,128)S(1)}, f32[8,256]{1,0:T(8,128)S(1)}) custom-call(s32[2,256]{1,0:T(2,128)} %bitcast.15, bf16[3,32,4096]{2,1,0:T(8,128)(2,1)} %bitcast.14, bf16[4000,4096]{1,0:T(8,128)(2,1)} %bitcast.12, f32[16000,128]{1,0:T(8,128)} %bitcast.13), custom_call_target="tpu_custom_call" | custom-call | tf_op jit(solution)/shard_map/pallas_call | solution.py:465
  94.3 5.2 %shard_map.76 = (f32[2,4000,256]{2,1,0:T(8,128)}, f32[4000,256]{1,0:T(8,128)}, f32[2,256]{1,0:T(2,128)}, f32[1,256]{1,0:T(1,128)}) custom-call(f32[3,4096,256]{2,1,0:T(8,128)S(1)} %get-tuple-element.10.z, f32[8,256]{1,0:T(8,128)S(1)} %get-tuple-element.11.small), custom_call_target="tpu_custom_call" | custom-call | tf_op jit(solution)/shard_map/pallas_call | solution.py:493

commit v5 on v3

--- a/solution.py
+++ b/solution.py
@@ -36,9 +36,10 @@
     drafts = positions - 1
     rows = batch // n
     vocab = w_ref.shape[0]
-    width = qall.shape[2]
-    seg = width // SEGS
+    seg = qall.shape[3]
+    width = seg * SEGS
     tiles = width // LANES
+    per = seg // LANES
     pitch = q_ref.shape[0] // rows
     all_tiles = pitch // drafts
     off = (k * vocab) % LANES
@@ -156,19 +157,19 @@
                         y = jnp.exp(0.25 * jnp.log(v) + rowc[i * (rows // 8) + g])
                         parts.append((y + 0.5).astype(jnp.int32) - HALF)
                     code = jnp.concatenate(parts, axis=0).astype(jnp.int16)
-                    put(i, gg, pl.ds(pl.multiple_of(j * LANES, LANES), LANES), code)
+                    put(i, gg, j // per, pl.ds(pl.multiple_of((j % per) * LANES, LANES), LANES), code)
             return 0
 
         lax.fori_loop(0, tiles, body, 0)
 
     def to_slot(r):
-        def put(i, gg, cols, code):
-            scode[r, i, 16 * gg:16 * gg + 16, cols] = code
+        def put(i, gg, s, cols, code):
+            scode[r, i, s, 16 * gg:16 * gg + 16, cols] = code
 
         return put
 
-    def to_self(i, gg, cols, code):
-        qall[i, pl.ds(pl.multiple_of(k * rows + 16 * gg, 16), 16), cols] = code
+    def to_self(i, gg, s, cols, code):
+        qall[i, s, pl.ds(pl.multiple_of(k * rows + 16 * gg, 16), 16), cols] = code
 
     encode(2 * far, to_slot(0))
     encode(2 * far + 1, to_slot(1))
@@ -190,12 +191,10 @@
     forward(2 * right + c, 1)
 
     def unit(buf_i, i, s):
-        return buf_i.at[i, :, pl.ds(pl.multiple_of(s * seg, LANES), seg)]
+        return buf_i.at[i, s]
 
     def landing(src, i, s):
-        return qall.at[
-            i, pl.ds(pl.multiple_of(src * rows, rows), rows), pl.ds(pl.multiple_of(s * seg, LANES), seg)
-        ]
+        return qall.at[i, s, pl.ds(pl.multiple_of(src * rows, rows), rows)]
 
     def direct(slot, i, s, who):
         return remote(
@@ -364,9 +363,24 @@
     def xmsg(p, i, src):
         return remote(mass.at[i, src], mass.at[i, src], x_send.at[i * n + p], x_recv.at[i * n + src], (k + p) % n)
 
+    def drain(u, _):
+        direct(u // 8, (u % 8) // SEGS, u % SEGS, mate).wait_send()
+        return 0
+
+    def drain_relay(v, _):
+        relay(0, v).wait_send()
+        relay(1, v).wait_send()
+        return 0
+
     for i in range(drafts):
         acc = [jnp.zeros((8, LANES), F32) for _ in range(batch // LANES)]
         for s in range(SEGS):
+            if i == drafts - 1 and s == SEGS - 1:
+                for cp in own_sends + [rel_r, rel_l] + fwd:
+                    cp.wait_send()
+                for p in range(1, n):
+                    msg(p, k).wait_send()
+                lax.fori_loop(0, 7 * 8, drain, 0)
             for p in range(1, n):
                 src = (k + p) % n
                 remote(
@@ -379,7 +393,7 @@
                 out = []
                 for h in range(batch // LANES):
                     ls = slice(h * LANES, (h + 1) * LANES)
-                    code = qall[i, ls, at].astype(jnp.int32).astype(F32)
+                    code = qall[i, s, ls, pl.ds(pl.multiple_of(t * LANES, LANES), LANES)].astype(jnp.int32).astype(F32)
                     y = code.T + float(HALF)
                     y = y * y
                     qt = y * y * q_scale[i:i + 1, ls]
@@ -393,6 +407,7 @@
             mass[i, k, :, h * LANES:(h + 1) * LANES] = acc[h]
         for p in range(1, n):
             xmsg(p, i, k).start()
+    lax.fori_loop(0, 8, drain_relay, 0)
     small_ref[...] = jnp.zeros(small_ref.shape, F32)
     small_ref[2:4, :] = p_pick
     small_ref[4:6, :] = q_pick
@@ -402,25 +417,9 @@
         total = jnp.sum(jnp.sum(mass[i], axis=0), axis=0, keepdims=True)
         small_ref[i:i + 1, :] = 1.0 / total
 
-    for cp in own_sends + [rel_r, rel_l] + fwd:
-        cp.wait_send()
     for p in range(1, n):
-        msg(p, k).wait_send()
         for i in range(drafts):
             xmsg(p, i, k).wait_send()
-
-    def drain(u, _):
-        direct(u // 8, (u % 8) // SEGS, u % SEGS, mate).wait_send()
-        return 0
-
-    lax.fori_loop(0, 7 * 8, drain, 0)
-
-    def drain_relay(v, _):
-        relay(0, v).wait_send()
-        relay(1, v).wait_send()
-        return 0
-
-    lax.fori_loop(0, 8, drain_relay, 0)
 
 
 def finish(n, z, small, res_ref, bonus_ref, acc_ref, exp_ref, buf, sem):
@@ -471,8 +470,8 @@
                 pltpu.VMEM((drafts, batch), jnp.int32),
                 pltpu.VMEM((positions, batch, dim), jnp.bfloat16),
                 pltpu.VMEM((rows * q_tiles * drafts, LANES), F32),
-                pltpu.VMEM((n - 1, drafts, rows, width), jnp.int16),
-                pltpu.VMEM((drafts, batch, width), jnp.int16),
+                pltpu.VMEM((n - 1, drafts, SEGS, rows, width // SEGS), jnp.int16),
+                pltpu.VMEM((drafts, SEGS, batch, width // SEGS), jnp.int16),
                 pltpu.VMEM((2, 8, rows, width // SEGS), jnp.int16),
                 pltpu.VMEM((2, vocab // STEPS, dim), jnp.bfloat16),
                 pltpu.VMEM((n, 16, batch), F32),

time: 94.2 us -> 94.1 us (level)
  no operation moved by 1% of the time
where the time goes in v5:
time: 94.1 us
  Pallas kernels  93.4 us (99%)
    pallas_call x1, Pallas kernels, local(): pl.pallas_call(functools.partial(kernel, n), out_shape=(jax.ShapeDtypeStr...  88.3 us
    pallas_call x1, Pallas kernels, local(): pl.pallas_call(functools.partial(finish, n), out_shape=(jax.ShapeDtypeStr...  5.17 us

profile of v5, /device:TPU:113, one launch (start us, length us, event | category | flops | bytes accessed | tf_op | source)
XLA Modules:
  0.0 94.1 jit_solution(2988535551064716431)
XLA Ops:
  0.6 88.3 %shard_map.75 = (f32[3,4096,256]{2,1,0:T(8,128)S(1)}, f32[8,256]{1,0:T(8,128)S(1)}) custom-call(s32[2,256]{1,0:T(2,128)} %bitcast.15, bf16[3,32,4096]{2,1,0:T(8,128)(2,1)} %bitcast.14, bf16[4000,4096]{1,0:T(8,128)(2,1)} %bitcast.12, f32[16000,128]{1,0:T(8,128)} %bitcast.13), custom_call_target="tpu_custom_call" | custom-call | tf_op jit(solution)/shard_map/pallas_call | solution.py:461
  88.9 5.2 %shard_map.76 = (f32[2,4000,256]{2,1,0:T(8,128)}, f32[4000,256]{1,0:T(8,128)}, f32[2,256]{1,0:T(2,128)}, f32[1,256]{1,0:T(1,128)}) custom-call(f32[3,4096,256]{2,1,0:T(8,128)S(1)} %get-tuple-element.10.z, f32[8,256]{1,0:T(8,128)S(1)} %get-tuple-element.11.small), custom_call_target="tpu_custom_call" | custom-call | tf_op jit(solution)/shard_map/pallas_call | solution.py:489

commit v6 on v5

--- a/solution.py
+++ b/solution.py
@@ -39,6 +39,7 @@
     seg = qall.shape[3]
     width = seg * SEGS
     tiles = width // LANES
+    units = drafts * SEGS
     per = seg // LANES
     pitch = q_ref.shape[0] // rows
     all_tiles = pitch // drafts
@@ -61,18 +62,15 @@
         part = pl.ds(g * 8 * pitch, 8 * pitch)
         return pltpu.make_async_copy(q_ref.at[part], stage.at[part], loc.at[1 + g])
 
-    for g in range(rows // 8):
-        stage_cp(g).start()
-
     def w_cp(t, slot):
         return pltpu.make_async_copy(
             w_ref.at[pl.ds(pl.multiple_of(t * wrows, 8), wrows)], wbuf.at[slot], wsem.at[slot]
         )
 
     barrier = pltpu.get_barrier_semaphore()
-    for p in range(1, n):
-        pl.semaphore_signal(barrier, inc=1, device_id={"tp": (k + p) % n}, device_id_type=MESH)
-    pl.semaphore_wait(barrier, n - 1)
+    for who in (2 * right + c, 2 * left + c, mate):
+        pl.semaphore_signal(barrier, inc=1, device_id={"tp": who}, device_id_type=MESH)
+    pl.semaphore_wait(barrier, 3)
 
     def hpiece(src, half):
         return hall.at[:, pl.ds(pl.multiple_of(src * rows, rows), rows), pl.ds(half * hcol, hcol)]
@@ -91,6 +89,8 @@
         cp = hcopy(k, half, h_send.at[idx], who)
         cp.start()
         own_sends.append(cp)
+    for g in range(rows // 8):
+        stage_cp(g).start()
     w_cp(0, 0).start()
     w_cp(1, 1).start()
 
@@ -199,28 +199,28 @@
     def direct(slot, i, s, who):
         return remote(
             unit(scode.at[slot], i, s), landing(k, i, s),
-            q_send.at[slot * 8 + i * SEGS + s], q_recv.at[k * 8 + i * SEGS + s], who,
+            q_send.at[slot * units + i * SEGS + s], q_recv.at[k * units + i * SEGS + s], who,
         )
 
     def out_far(way, v):
-        i, s, cc = v // 4, 2 * ((v // 2) % 2) + way, v % 2
+        i, s, cc = v // SEGS, 2 * ((v // 2) % (SEGS // 2)) + way, v % 2
         who = 2 * (right if way == 0 else left) + c
         return remote(
             unit(scode.at[cc], i, s), rbuf.at[way, v],
-            q_send.at[cc * 8 + i * SEGS + s], r_recv.at[way * 8 + v], who,
+            q_send.at[cc * units + i * SEGS + s], r_recv.at[way * units + v], who,
         )
 
     def relay(way, v):
-        i, s, cc = v // 4, 2 * ((v // 2) % 2) + way, v % 2
+        i, s, cc = v // SEGS, 2 * ((v // 2) % (SEGS // 2)) + way, v % 2
         src = 2 * (left if way == 0 else right) + c
         who = 2 * (right if way == 0 else left) + cc
         return remote(
             rbuf.at[way, v], landing(src, i, s),
-            r_send.at[way * 8 + v], q_recv.at[src * 8 + i * SEGS + s], who,
+            r_send.at[way * units + v], q_recv.at[src * units + i * SEGS + s], who,
         )
 
     def near(way, u):
-        i, s, cc = u // 8, (u // 2) % SEGS, u % 2
+        i, s, cc = u // (2 * SEGS), (u // 2) % SEGS, u % 2
         who = 2 * (right if way == 0 else left) + cc
         return direct(2 + 2 * way + cc, i, s, who)
 
@@ -255,8 +255,8 @@
         send_near(u)
         return 0
 
-    lax.fori_loop(0, 4, first_far, 0)
-    lax.fori_loop(0, 8, first_near, 0)
+    lax.fori_loop(0, SEGS, first_far, 0)
+    lax.fori_loop(0, 2 * SEGS, first_near, 0)
     encode(mate, to_slot(6))
     encode(k, to_self)
 
@@ -279,18 +279,18 @@
 
         @pl.when((t >= 2) & (t < 4))
         def _():
-            pass_on(2 * (t - 2))
-            pass_on(2 * (t - 2) + 1)
+            for e in range(SEGS // 2):
+                pass_on((SEGS // 2) * (t - 2) + e)
 
         @pl.when((t >= 4) & (t < 6))
         def _():
-            send_far(4 + 2 * (t - 4))
-            send_far(4 + 2 * (t - 4) + 1)
+            for e in range(SEGS // 2):
+                send_far(SEGS + (SEGS // 2) * (t - 4) + e)
 
         @pl.when(t >= 6)
         def _():
-            send_near(8 + 2 * (t - 6))
-            send_near(8 + 2 * (t - 6) + 1)
+            for e in range(SEGS // 2):
+                send_near(2 * SEGS + (SEGS // 2) * (t - 6) + e)
 
         w_cp(t, slot).wait()
         prod = INV_TEMP * lax.dot_general(
@@ -339,7 +339,7 @@
     for p in range(1, n):
         msg(p, k).start()
 
-    for v in range(4, 8):
+    for v in range(SEGS, 2 * SEGS):
         pass_on(v)
     for p in range(1, n):
         msg(p, (k + p) % n).wait_recv()
@@ -364,7 +364,7 @@
         return remote(mass.at[i, src], mass.at[i, src], x_send.at[i * n + p], x_recv.at[i * n + src], (k + p) % n)
 
     def drain(u, _):
-        direct(u // 8, (u % 8) // SEGS, u % SEGS, mate).wait_send()
+        direct(u // units, (u % units) // SEGS, u % SEGS, mate).wait_send()
         return 0
 
     def drain_relay(v, _):
@@ -380,12 +380,12 @@
                     cp.wait_send()
                 for p in range(1, n):
                     msg(p, k).wait_send()
-                lax.fori_loop(0, 7 * 8, drain, 0)
+                lax.fori_loop(0, (n - 1) * units, drain, 0)
             for p in range(1, n):
                 src = (k + p) % n
                 remote(
                     landing(src, i, s), landing(src, i, s), q_send.at[0],
-                    q_recv.at[src * 8 + i * SEGS + s], mate,
+                    q_recv.at[src * units + i * SEGS + s], mate,
                 ).wait_recv()
 
             def body(t, acc, i=i, s=s):
@@ -404,17 +404,17 @@
 
             acc = lax.fori_loop(0, tiles // SEGS, body, tuple(acc))
         for h in range(batch // LANES):
-            mass[i, k, :, h * LANES:(h + 1) * LANES] = acc[h]
+            mass[i, k, :, h * LANES:(h + 1) * LANES] = jnp.sum(acc[h], axis=0, keepdims=True)
         for p in range(1, n):
             xmsg(p, i, k).start()
-    lax.fori_loop(0, 8, drain_relay, 0)
+    lax.fori_loop(0, units, drain_relay, 0)
     small_ref[...] = jnp.zeros(small_ref.shape, F32)
     small_ref[2:4, :] = p_pick
     small_ref[4:6, :] = q_pick
     for i in range(drafts):
         for p in range(1, n):
             xmsg(p, i, (k + p) % n).wait_recv()
-        total = jnp.sum(jnp.sum(mass[i], axis=0), axis=0, keepdims=True)
+        total = jnp.sum(mass[i], axis=0)
         small_ref[i:i + 1, :] = 1.0 / total
 
     for p in range(1, n):
@@ -472,13 +472,13 @@
                 pltpu.VMEM((rows * q_tiles * drafts, LANES), F32),
                 pltpu.VMEM((n - 1, drafts, SEGS, rows, width // SEGS), jnp.int16),
                 pltpu.VMEM((drafts, SEGS, batch, width // SEGS), jnp.int16),
-                pltpu.VMEM((2, 8, rows, width // SEGS), jnp.int16),
+                pltpu.VMEM((2, drafts * SEGS, rows, width // SEGS), jnp.int16),
                 pltpu.VMEM((2, vocab // STEPS, dim), jnp.bfloat16),
                 pltpu.VMEM((n, 16, batch), F32),
-                pltpu.VMEM((drafts, n, 8, batch), F32),
+                pltpu.VMEM((drafts, n, 1, batch), F32),
                 pltpu.VMEM((drafts * (rows // 8), 8, LANES), F32),
                 dma((8,)), dma((8,)), dma((2 * n,)),
-                dma((7 * 8,)), dma((8 * 8,)), dma((16,)), dma((16,)),
+                dma((n * drafts * SEGS,)), dma((n * drafts * SEGS,)), dma((2 * drafts * SEGS,)), dma((2 * drafts * SEGS,)),
                 dma((n,)), dma((n,)), dma((2 * n,)), dma((2 * n,)),
                 dma((8,)), dma((2,)),
             ],

time: 94.1 us -> 93.8 us (level)
  no operation moved by 1% of the time
where the time goes in v6:
time: 93.8 us; the launch traced here: 93.7 us
  Pallas kernels  93.1 us (99%)
    pallas_call x1, Pallas kernels, local(): pl.pallas_call(functools.partial(kernel, n), out_shape=(jax.ShapeDtypeStr...  87.9 us
    pallas_call x1, Pallas kernels, local(): pl.pallas_call(functools.partial(finish, n), out_shape=(jax.ShapeDtypeStr...  5.17 us

profile of v6, /device:TPU:113, one launch (start us, length us, event | category | flops | bytes accessed | tf_op | source)
XLA Modules:
  0.0 93.7 jit_solution(1473744262061095826)
XLA Ops:
  0.6 87.9 %shard_map.75 = (f32[3,4096,256]{2,1,0:T(8,128)S(1)}, f32[8,256]{1,0:T(8,128)S(1)}) custom-call(s32[2,256]{1,0:T(2,128)} %bitcast.15, bf16[3,32,4096]{2,1,0:T(8,128)(2,1)} %bitcast.14, bf16[4000,4096]{1,0:T(8,128)(2,1)} %bitcast.12, f32[16000,128]{1,0:T(8,128)} %bitcast.13), custom_call_target="tpu_custom_call" | custom-call | tf_op jit(solution)/shard_map/pallas_call | solution.py:461
  88.6 5.2 %shard_map.76 = (f32[2,4000,256]{2,1,0:T(8,128)}, f32[4000,256]{1,0:T(8,128)}, f32[2,256]{1,0:T(2,128)}, f32[1,256]{1,0:T(1,128)}) custom-call(f32[3,4096,256]{2,1,0:T(8,128)S(1)} %get-tuple-element.10.z, f32[8,256]{1,0:T(8,128)S(1)} %get-tuple-element.11.small), custom_call_target="tpu_custom_call" | custom-call | tf_op jit(solution)/shard_map/pallas_call | solution.py:489

commit v7 on v6

--- a/solution.py
+++ b/solution.py
@@ -12,7 +12,7 @@
 TOP = 65535.0
 HALF = 32768
 LANES = 128
-SEGS = 4
+SEGS = 2
 STEPS = 10
 PARTS = 5
 F32 = jnp.float32

time: 93.8 us -> 92.5 us (0.986)
  Pallas kernels: 93.1 us -> 91.8 us
    pallas_call x1, Pallas kernels: 87.9 us -> 86.6 us  [local(): pl.pallas_call(functools.partial(kernel, n), out_shape=(jax.ShapeDtypeStr...]
where the time goes in v7:
time: 92.5 us; the launch traced here: 92.4 us
  Pallas kernels  91.8 us (99%)
    pallas_call x1, Pallas kernels, local(): pl.pallas_call(functools.partial(kernel, n), out_shape=(jax.ShapeDtypeStr...  86.6 us
    pallas_call x1, Pallas kernels, local(): pl.pallas_call(functools.partial(finish, n), out_shape=(jax.ShapeDtypeStr...  5.17 us

profile of v7, /device:TPU:113, one launch (start us, length us, event | category | flops | bytes accessed | tf_op | source)
XLA Modules:
  0.0 92.4 jit_solution(12883796751742867730)
XLA Ops:
  0.6 86.6 %shard_map.75 = (f32[3,4096,256]{2,1,0:T(8,128)S(1)}, f32[8,256]{1,0:T(8,128)S(1)}) custom-call(s32[2,256]{1,0:T(2,128)} %bitcast.15, bf16[3,32,4096]{2,1,0:T(8,128)(2,1)} %bitcast.14, bf16[4000,4096]{1,0:T(8,128)(2,1)} %bitcast.12, f32[16000,128]{1,0:T(8,128)} %bitcast.13), custom_call_target="tpu_custom_call" | custom-call | tf_op jit(solution)/shard_map/pallas_call | solution.py:461
  87.2 5.2 %shard_map.76 = (f32[2,4000,256]{2,1,0:T(8,128)}, f32[4000,256]{1,0:T(8,128)}, f32[2,256]{1,0:T(2,128)}, f32[1,256]{1,0:T(1,128)}) custom-call(f32[3,4096,256]{2,1,0:T(8,128)S(1)} %get-tuple-element.10.z, f32[8,256]{1,0:T(8,128)S(1)} %get-tuple-element.11.small), custom_call_target="tpu_custom_call" | custom-call | tf_op jit(solution)/shard_map/pallas_call | solution.py:489

commit v8 on v6

--- a/solution.py
+++ b/solution.py
@@ -13,6 +13,7 @@
 HALF = 32768
 LANES = 128
 SEGS = 4
+PIECES = (((0, 4),), ((0, 2), (2, 1), (3, 1)))
 STEPS = 10
 PARTS = 5
 F32 = jnp.float32
@@ -190,52 +191,50 @@
     rel_l.start()
     forward(2 * right + c, 1)
 
-    def unit(buf_i, i, s):
-        return buf_i.at[i, s]
-
-    def landing(src, i, s):
-        return qall.at[i, s, pl.ds(pl.multiple_of(src * rows, rows), rows)]
-
-    def direct(slot, i, s, who):
+    def landing(src, i, s, count):
+        return qall.at[i, pl.ds(s, count), pl.ds(pl.multiple_of(src * rows, rows), rows)]
+
+    def direct(slot, i, who):
         return remote(
-            unit(scode.at[slot], i, s), landing(k, i, s),
-            q_send.at[slot * units + i * SEGS + s], q_recv.at[k * units + i * SEGS + s], who,
-        )
-
-    def out_far(way, v):
-        i, s, cc = v // SEGS, 2 * ((v // 2) % (SEGS // 2)) + way, v % 2
+            scode.at[slot, i], landing(k, i, 0, SEGS),
+            q_send.at[slot * drafts + i], q_recv.at[k * units + i * SEGS], who,
+        )
+
+    def out_far(way, i):
         who = 2 * (right if way == 0 else left) + c
         return remote(
-            unit(scode.at[cc], i, s), rbuf.at[way, v],
-            q_send.at[cc * units + i * SEGS + s], r_recv.at[way * units + v], who,
-        )
-
-    def relay(way, v):
-        i, s, cc = v // SEGS, 2 * ((v // 2) % (SEGS // 2)) + way, v % 2
+            scode.at[way, i], rbuf.at[way, i],
+            q_send.at[way * drafts + i], r_recv.at[way * drafts + i], who,
+        )
+
+    def relay(way, i, s, count):
         src = 2 * (left if way == 0 else right) + c
-        who = 2 * (right if way == 0 else left) + cc
+        who = 2 * (right if way == 0 else left) + way
         return remote(
-            rbuf.at[way, v], landing(src, i, s),
-            r_send.at[way * units + v], q_recv.at[src * units + i * SEGS + s], who,
-        )
-
-    def near(way, u):
-        i, s, cc = u // (2 * SEGS), (u // 2) % SEGS, u % 2
-        who = 2 * (right if way == 0 else left) + cc
-        return direct(2 + 2 * way + cc, i, s, who)
-
-    def send_far(v):
-        out_far(0, v).start()
-        out_far(1, v).start()
-
-    def send_near(u):
-        near(0, u).start()
-        near(1, u).start()
-
-    def pass_on(v):
+            rbuf.at[way, i, pl.ds(s, count)], landing(src, i, s, count),
+            r_send.at[way * units + i * SEGS + s], q_recv.at[src * units + i * SEGS + s], who,
+        )
+
+    def send_far(i):
+        out_far(0, i).start()
+        out_far(1, i).start()
+
+    def send_near(i, cc):
+        direct(2 + cc, i, 2 * right + cc).start()
+        direct(4 + cc, i, 2 * left + cc).start()
+
+    def pass_on(i):
         for way in range(2):
-            out_far(way, v).wait_recv()
-            relay(way, v).start()
+            out_far(way, i).wait_recv()
+        for s, count in PIECES[i]:
+            for way in range(2):
+                relay(way, i, s, count).start()
+
+    def landed(src, i, s, count):
+        remote(
+            landing(src, i, s, count), landing(src, i, s, count), q_send.at[0],
+            q_recv.at[src * units + i * SEGS + s], mate,
+        ).wait_recv()
 
     encode(2 * right, to_slot(2))
     encode(2 * right + 1, to_slot(3))
@@ -247,24 +246,14 @@
     hwait(2 * right + c, 0)
     forward(2 * right + c, 0)
 
-    def first_far(v, _):
-        send_far(v)
-        return 0
-
-    def first_near(u, _):
-        send_near(u)
-        return 0
-
-    lax.fori_loop(0, SEGS, first_far, 0)
-    lax.fori_loop(0, 2 * SEGS, first_near, 0)
+    send_far(0)
+    send_near(0, 0)
+    send_near(0, 1)
     encode(mate, to_slot(6))
     encode(k, to_self)
 
-    def to_mate(u, _):
-        direct(6, u // SEGS, u % SEGS, mate).start()
-        return 0
-
-    lax.fori_loop(0, drafts * SEGS, to_mate, 0)
+    for i in range(drafts):
+        direct(6, i, mate).start()
 
     hwait(2 * far + c, 0)
     forward(2 * far + c, 0)
@@ -277,20 +266,21 @@
     def step(t, top):
         slot = t % 2
 
-        @pl.when((t >= 2) & (t < 4))
+        @pl.when(t == 2)
         def _():
-            for e in range(SEGS // 2):
-                pass_on((SEGS // 2) * (t - 2) + e)
-
-        @pl.when((t >= 4) & (t < 6))
+            pass_on(0)
+
+        @pl.when(t == 4)
         def _():
-            for e in range(SEGS // 2):
-                send_far(SEGS + (SEGS // 2) * (t - 4) + e)
-
-        @pl.when(t >= 6)
+            send_far(1)
+
+        @pl.when(t == 6)
         def _():
-            for e in range(SEGS // 2):
-                send_near(2 * SEGS + (SEGS // 2) * (t - 6) + e)
+            send_near(1, 0)
+
+        @pl.when(t == 7)
+        def _():
+            send_near(1, 1)
 
         w_cp(t, slot).wait()
         prod = INV_TEMP * lax.dot_general(
@@ -339,8 +329,7 @@
     for p in range(1, n):
         msg(p, k).start()
 
-    for v in range(SEGS, 2 * SEGS):
-        pass_on(v)
+    pass_on(1)
     for p in range(1, n):
         msg(p, (k + p) % n).wait_recv()
 
@@ -363,37 +352,29 @@
     def xmsg(p, i, src):
         return remote(mass.at[i, src], mass.at[i, src], x_send.at[i * n + p], x_recv.at[i * n + src], (k + p) % n)
 
-    def drain(u, _):
-        direct(u // units, (u % units) // SEGS, u % SEGS, mate).wait_send()
-        return 0
-
-    def drain_relay(v, _):
-        relay(0, v).wait_send()
-        relay(1, v).wait_send()
-        return 0
-
-    for i in range(drafts):
-        acc = [jnp.zeros((8, LANES), F32) for _ in range(batch // LANES)]
-        for s in range(SEGS):
-            if i == drafts - 1 and s == SEGS - 1:
+    near_srcs = [2 * right, 2 * right + 1, 2 * left, 2 * left + 1, mate]
+    for i in range(drafts):
+        acc = tuple(jnp.zeros((8, LANES), F32) for _ in range(batch // LANES))
+        for src in near_srcs:
+            landed(src, i, 0, SEGS)
+        for s, count in PIECES[i]:
+            if i == drafts - 1 and s > 0 and s + count == SEGS:
                 for cp in own_sends + [rel_r, rel_l] + fwd:
                     cp.wait_send()
                 for p in range(1, n):
                     msg(p, k).wait_send()
-                lax.fori_loop(0, (n - 1) * units, drain, 0)
-            for p in range(1, n):
-                src = (k + p) % n
-                remote(
-                    landing(src, i, s), landing(src, i, s), q_send.at[0],
-                    q_recv.at[src * units + i * SEGS + s], mate,
-                ).wait_recv()
+                for u in range((n - 1) * drafts):
+                    direct(u // drafts, u % drafts, mate).wait_send()
+            for cc in range(2):
+                landed(2 * far + cc, i, s, count)
 
             def body(t, acc, i=i, s=s):
-                at = pl.ds(pl.multiple_of((s * (tiles // SEGS) + t) * LANES, LANES), LANES)
+                at = pl.ds(pl.multiple_of((s * per + t) * LANES, LANES), LANES)
+                sub = pl.ds(pl.multiple_of((t % per) * LANES, LANES), LANES)
                 out = []
                 for h in range(batch // LANES):
                     ls = slice(h * LANES, (h + 1) * LANES)
-                    code = qall[i, s, ls, pl.ds(pl.multiple_of(t * LANES, LANES), LANES)].astype(jnp.int32).astype(F32)
+                    code = qall[i, s + t // per, ls, sub].astype(jnp.int32).astype(F32)
                     y = code.T + float(HALF)
                     y = y * y
                     qt = y * y * q_scale[i:i + 1, ls]
@@ -402,12 +383,15 @@
                     out.append(acc[h] + jnp.sum(ex.reshape(LANES // 8, 8, LANES), axis=0))
                 return tuple(out)
 
-            acc = lax.fori_loop(0, tiles // SEGS, body, tuple(acc))
+            acc = lax.fori_loop(0, count * per, body, acc)
         for h in range(batch // LANES):
             mass[i, k, :, h * LANES:(h + 1) * LANES] = jnp.sum(acc[h], axis=0, keepdims=True)
         for p in range(1, n):
             xmsg(p, i, k).start()
-    lax.fori_loop(0, units, drain_relay, 0)
+    for i in range(drafts):
+        for s, count in PIECES[i]:
+            for way in range(2):
+                relay(way, i, s, count).wait_send()
     small_ref[...] = jnp.zeros(small_ref.shape, F32)
     small_ref[2:4, :] = p_pick
     small_ref[4:6, :] = q_pick
@@ -472,7 +456,7 @@
                 pltpu.VMEM((rows * q_tiles * drafts, LANES), F32),
                 pltpu.VMEM((n - 1, drafts, SEGS, rows, width // SEGS), jnp.int16),
                 pltpu.VMEM((drafts, SEGS, batch, width // SEGS), jnp.int16),
-                pltpu.VMEM((2, drafts * SEGS, rows, width // SEGS), jnp.int16),
+                pltpu.VMEM((2, drafts, SEGS, rows, width // SEGS), jnp.int16),
                 pltpu.VMEM((2, vocab // STEPS, dim), jnp.bfloat16),
                 pltpu.VMEM((n, 16, batch), F32),
                 pltpu.VMEM((drafts, n, 1, batch), F32),

time: 93.8 us -> 93 us (level)
  no operation moved by 1% of the time
where the time goes in v8:
time: 93 us; the launch traced here: 92.9 us
  Pallas kernels  92.3 us (99%)
    pallas_call x1, Pallas kernels, local(): pl.pallas_call(functools.partial(kernel, n), out_shape=(jax.ShapeDtypeStr...  87.1 us
    pallas_call x1, Pallas kernels, local(): pl.pallas_call(functools.partial(finish, n), out_shape=(jax.ShapeDtypeStr...  5.17 us

profile of v8, /device:TPU:113, one launch (start us, length us, event | category | flops | bytes accessed | tf_op | source)
XLA Modules:
  0.0 92.9 jit_solution(17464886745250672396)
XLA Ops:
  0.6 87.1 %shard_map.75 = (f32[3,4096,256]{2,1,0:T(8,128)S(1)}, f32[8,256]{1,0:T(8,128)S(1)}) custom-call(s32[2,256]{1,0:T(2,128)} %bitcast.15, bf16[3,32,4096]{2,1,0:T(8,128)(2,1)} %bitcast.14, bf16[4000,4096]{1,0:T(8,128)(2,1)} %bitcast.12, f32[16000,128]{1,0:T(8,128)} %bitcast.13), custom_call_target="tpu_custom_call" | custom-call | tf_op jit(solution)/shard_map/pallas_call | solution.py:445
  87.7 5.2 %shard_map.76 = (f32[2,4000,256]{2,1,0:T(8,128)}, f32[4000,256]{1,0:T(8,128)}, f32[2,256]{1,0:T(2,128)}, f32[1,256]{1,0:T(1,128)}) custom-call(f32[3,4096,256]{2,1,0:T(8,128)S(1)} %get-tuple-element.10.z, f32[8,256]{1,0:T(8,128)S(1)} %get-tuple-element.11.small), custom_call_target="tpu_custom_call" | custom-call | tf_op jit(solution)/shard_map/pallas_call | solution.py:473

commit v9 on v8

--- a/solution.py
+++ b/solution.py
@@ -200,16 +200,19 @@
             q_send.at[slot * drafts + i], q_recv.at[k * units + i * SEGS], who,
         )
 
+    def core_of(way):
+        return c if way == 0 else 1 - c
+
     def out_far(way, i):
         who = 2 * (right if way == 0 else left) + c
         return remote(
-            scode.at[way, i], rbuf.at[way, i],
-            q_send.at[way * drafts + i], r_recv.at[way * drafts + i], who,
+            scode.at[core_of(way), i], rbuf.at[way, i],
+            q_send.at[core_of(way) * drafts + i], r_recv.at[way * drafts + i], who,
         )
 
     def relay(way, i, s, count):
         src = 2 * (left if way == 0 else right) + c
-        who = 2 * (right if way == 0 else left) + way
+        who = 2 * (right if way == 0 else left) + core_of(way)
         return remote(
             rbuf.at[way, i, pl.ds(s, count)], landing(src, i, s, count),
             r_send.at[way * units + i * SEGS + s], q_recv.at[src * units + i * SEGS + s], who,
@@ -247,8 +250,8 @@
     forward(2 * right + c, 0)
 
     send_far(0)
-    send_near(0, 0)
-    send_near(0, 1)
+    send_near(0, c)
+    send_near(0, 1 - c)
     encode(mate, to_slot(6))
     encode(k, to_self)
 
@@ -276,11 +279,11 @@
 
         @pl.when(t == 6)
         def _():
-            send_near(1, 0)
+            send_near(1, c)
 
         @pl.when(t == 7)
         def _():
-            send_near(1, 1)
+            send_near(1, 1 - c)
 
         w_cp(t, slot).wait()
         prod = INV_TEMP * lax.dot_general(

time: 93 us -> 93 us (level)
  no operation moved by 1% of the time
where the time goes in v9:
time: 93 us; the launch traced here: 92.9 us
  Pallas kernels  92.3 us (99%)
    pallas_call x1, Pallas kernels, local(): pl.pallas_call(functools.partial(kernel, n), out_shape=(jax.ShapeDtypeStr...  87.1 us
    pallas_call x1, Pallas kernels, local(): pl.pallas_call(functools.partial(finish, n), out_shape=(jax.ShapeDtypeStr...  5.17 us

profile of v9, /device:TPU:113, one launch (start us, length us, event | category | flops | bytes accessed | tf_op | source)
XLA Modules:
  0.0 92.9 jit_solution(9706966410720124058)
XLA Ops:
  0.6 87.1 %shard_map.75 = (f32[3,4096,256]{2,1,0:T(8,128)S(1)}, f32[8,256]{1,0:T(8,128)S(1)}) custom-call(s32[2,256]{1,0:T(2,128)} %bitcast.15, bf16[3,32,4096]{2,1,0:T(8,128)(2,1)} %bitcast.14, bf16[4000,4096]{1,0:T(8,128)(2,1)} %bitcast.12, f32[16000,128]{1,0:T(8,128)} %bitcast.13), custom_call_target="tpu_custom_call" | custom-call | tf_op jit(solution)/shard_map/pallas_call | solution.py:448
  87.7 5.2 %shard_map.76 = (f32[2,4000,256]{2,1,0:T(8,128)}, f32[4000,256]{1,0:T(8,128)}, f32[2,256]{1,0:T(2,128)}, f32[1,256]{1,0:T(1,128)}) custom-call(f32[3,4096,256]{2,1,0:T(8,128)S(1)} %get-tuple-element.10.z, f32[8,256]{1,0:T(8,128)S(1)} %get-tuple-element.11.small), custom_call_target="tpu_custom_call" | custom-call | tf_op jit(solution)/shard_map/pallas_call | solution.py:476

commit v10 on v9

--- a/solution.py
+++ b/solution.py
@@ -85,11 +85,12 @@
     hid_cp.wait()
     own_sends = []
     for idx, (who, half) in enumerate(
-        [(2 * right + c, 0), (2 * left + c, 1), (2 * right + c, 1), (2 * left + c, 0), (mate, 0), (mate, 1)]
+        [(2 * right + c, 0), (2 * left + c, 1), (mate, 0), (mate, 1), (2 * right + c, 1), (2 * left + c, 0)]
     ):
         cp = hcopy(k, half, h_send.at[idx], who)
+        own_sends.append(cp)
+    for cp in own_sends[:4]:
         cp.start()
-        own_sends.append(cp)
     for g in range(rows // 8):
         stage_cp(g).start()
     w_cp(0, 0).start()
@@ -182,6 +183,10 @@
         cp.start()
         fwd.append(cp)
 
+    own_sends[0].wait_send()
+    own_sends[4].start()
+    own_sends[1].wait_send()
+    own_sends[5].start()
     hwait(2 * left + c, 0)
     rel_r = hcopy(2 * left + c, 0, h_send.at[6], 2 * right + c)
     rel_r.start()
@@ -244,20 +249,18 @@
     encode(2 * left, to_slot(4))
     encode(2 * left + 1, to_slot(5))
 
+    encode(mate, to_slot(6))
+    encode(k, to_self)
+    for cp in own_sends[4:6]:
+        cp.wait_send()
+    send_far(0)
+    send_far(1)
+    for i in range(drafts):
+        direct(6, i, mate).start()
     hwait(2 * left + c, 1)
     forward(2 * left + c, 1)
     hwait(2 * right + c, 0)
     forward(2 * right + c, 0)
-
-    send_far(0)
-    send_near(0, c)
-    send_near(0, 1 - c)
-    encode(mate, to_slot(6))
-    encode(k, to_self)
-
-    for i in range(drafts):
-        direct(6, i, mate).start()
-
     hwait(2 * far + c, 0)
     forward(2 * far + c, 0)
     hwait(2 * far + c, 1)
@@ -269,21 +272,15 @@
     def step(t, top):
         slot = t % 2
 
-        @pl.when(t == 2)
-        def _():
-            pass_on(0)
-
-        @pl.when(t == 4)
-        def _():
-            send_far(1)
-
-        @pl.when(t == 6)
-        def _():
-            send_near(1, c)
-
-        @pl.when(t == 7)
-        def _():
-            send_near(1, 1 - c)
+        for when, act in (
+            (1, lambda: send_near(0, c)),
+            (3, lambda: send_near(0, 1 - c)),
+            (5, lambda: pass_on(0)),
+            (6, lambda: send_near(1, c)),
+            (8, lambda: pass_on(1)),
+            (9, lambda: send_near(1, 1 - c)),
+        ):
+            pl.when(t == when)(act)
 
         w_cp(t, slot).wait()
         prod = INV_TEMP * lax.dot_general(
@@ -332,7 +329,6 @@
     for p in range(1, n):
         msg(p, k).start()
 
-    pass_on(1)
     for p in range(1, n):
         msg(p, (k + p) % n).wait_recv()
 
@@ -362,7 +358,7 @@
             landed(src, i, 0, SEGS)
         for s, count in PIECES[i]:
             if i == drafts - 1 and s > 0 and s + count == SEGS:
-                for cp in own_sends + [rel_r, rel_l] + fwd:
+                for cp in own_sends[2:4] + [rel_r, rel_l] + fwd:
                     cp.wait_send()
                 for p in range(1, n):
                     msg(p, k).wait_send()

time: 93 us -> 97.7 us (1.051)
  Pallas kernels: 92.3 us -> 97 us
    pallas_call x1, Pallas kernels: 87.1 us -> 91.8 us  [local(): pl.pallas_call(functools.partial(kernel, n), out_shape=(jax.ShapeDtypeStr...]
where the time goes in v10:
time: 97.7 us; the launch traced here: 97.6 us
  Pallas kernels  97 us (99%)
    pallas_call x1, Pallas kernels, local(): pl.pallas_call(functools.partial(kernel, n), out_shape=(jax.ShapeDtypeStr...  91.8 us
    pallas_call x1, Pallas kernels, local(): pl.pallas_call(functools.partial(finish, n), out_shape=(jax.ShapeDtypeStr...  5.17 us

profile of v10, /device:TPU:113, one launch (start us, length us, event | category | flops | bytes accessed | tf_op | source)
XLA Modules:
  0.0 97.6 jit_solution(16773369467137166447)
XLA Ops:
  0.6 91.8 %shard_map.75 = (f32[3,4096,256]{2,1,0:T(8,128)S(1)}, f32[8,256]{1,0:T(8,128)S(1)}) custom-call(s32[2,256]{1,0:T(2,128)} %bitcast.15, bf16[3,32,4096]{2,1,0:T(8,128)(2,1)} %bitcast.14, bf16[4000,4096]{1,0:T(8,128)(2,1)} %bitcast.12, f32[16000,128]{1,0:T(8,128)} %bitcast.13), custom_call_target="tpu_custom_call" | custom-call | tf_op jit(solution)/shard_map/pallas_call | solution.py:444
  92.5 5.2 %shard_map.76 = (f32[2,4000,256]{2,1,0:T(8,128)}, f32[4000,256]{1,0:T(8,128)}, f32[2,256]{1,0:T(2,128)}, f32[1,256]{1,0:T(1,128)}) custom-call(f32[3,4096,256]{2,1,0:T(8,128)S(1)} %get-tuple-element.10.z, f32[8,256]{1,0:T(8,128)S(1)} %get-tuple-element.11.small), custom_call_target="tpu_custom_call" | custom-call | tf_op jit(solution)/shard_map/pallas_call | solution.py:472

commit v11 on v10

--- a/solution.py
+++ b/solution.py
@@ -25,7 +25,7 @@
     z, small_ref,
     tok_ref, hall, stage, scode, qall, rbuf, wbuf, msgs, mass, rowc,
     h_send, h_fwd, h_recv, q_send, q_recv, r_send, r_recv,
-    m_send, m_recv, x_send, x_recv, loc, wsem,
+    m_send, m_recv, x_send, x_recv, loc, wsem, p_send,
 ):
     k = lax.axis_index("tp")
     x, c = k // 2, k % 2
@@ -227,6 +227,18 @@
         out_far(0, i).start()
         out_far(1, i).start()
 
+    def piece(slot, s, count, who):
+        i = drafts - 1
+        return remote(
+            scode.at[slot, i, pl.ds(s, count)], landing(k, i, s, count),
+            p_send.at[slot * SEGS + s], q_recv.at[k * units + i * SEGS + s], who,
+        )
+
+    def last_pieces():
+        for s, count in PIECES[drafts - 1]:
+            yield piece(2 + 1 - c, s, count, 2 * right + 1 - c)
+            yield piece(4 + 1 - c, s, count, 2 * left + 1 - c)
+
     def send_near(i, cc):
         direct(2 + cc, i, 2 * right + cc).start()
         direct(4 + cc, i, 2 * left + cc).start()
@@ -234,9 +246,8 @@
     def pass_on(i):
         for way in range(2):
             out_far(way, i).wait_recv()
-        for s, count in PIECES[i]:
-            for way in range(2):
-                relay(way, i, s, count).start()
+        for way in range(2):
+            relay(way, i, 0, SEGS).start()
 
     def landed(src, i, s, count):
         remote(
@@ -278,7 +289,6 @@
             (5, lambda: pass_on(0)),
             (6, lambda: send_near(1, c)),
             (8, lambda: pass_on(1)),
-            (9, lambda: send_near(1, 1 - c)),
         ):
             pl.when(t == when)(act)
 
@@ -329,6 +339,8 @@
     for p in range(1, n):
         msg(p, k).start()
 
+    for cp in last_pieces():
+        cp.start()
     for p in range(1, n):
         msg(p, (k + p) % n).wait_recv()
 
@@ -351,10 +363,11 @@
     def xmsg(p, i, src):
         return remote(mass.at[i, src], mass.at[i, src], x_send.at[i * n + p], x_recv.at[i * n + src], (k + p) % n)
 
-    near_srcs = [2 * right, 2 * right + 1, 2 * left, 2 * left + 1, mate]
+    whole = [[2 * chip + cc for chip in (left, right, far) for cc in range(2)] + [mate], []]
+    whole[1] = [2 * left + c, 2 * right + c, 2 * far, 2 * far + 1, mate]
     for i in range(drafts):
         acc = tuple(jnp.zeros((8, LANES), F32) for _ in range(batch // LANES))
-        for src in near_srcs:
+        for src in whole[i]:
             landed(src, i, 0, SEGS)
         for s, count in PIECES[i]:
             if i == drafts - 1 and s > 0 and s + count == SEGS:
@@ -362,10 +375,14 @@
                     cp.wait_send()
                 for p in range(1, n):
                     msg(p, k).wait_send()
-                for u in range((n - 1) * drafts):
-                    direct(u // drafts, u % drafts, mate).wait_send()
-            for cc in range(2):
-                landed(2 * far + cc, i, s, count)
+                for slot in (0, 1, 2 + c, 4 + c, 6):
+                    for ii in range(drafts):
+                        direct(slot, ii, mate).wait_send()
+                for slot in (2 + 1 - c, 4 + 1 - c):
+                    direct(slot, 0, mate).wait_send()
+            if i == drafts - 1:
+                for chip in (left, right):
+                    landed(2 * chip + 1 - c, i, s, count)
 
             def body(t, acc, i=i, s=s):
                 at = pl.ds(pl.multiple_of((s * per + t) * LANES, LANES), LANES)
@@ -388,9 +405,10 @@
         for p in range(1, n):
             xmsg(p, i, k).start()
     for i in range(drafts):
-        for s, count in PIECES[i]:
-            for way in range(2):
-                relay(way, i, s, count).wait_send()
+        for way in range(2):
+            relay(way, i, 0, SEGS).wait_send()
+    for cp in last_pieces():
+        cp.wait_send()
     small_ref[...] = jnp.zeros(small_ref.shape, F32)
     small_ref[2:4, :] = p_pick
     small_ref[4:6, :] = q_pick
@@ -463,7 +481,7 @@
                 dma((8,)), dma((8,)), dma((2 * n,)),
                 dma((n * drafts * SEGS,)), dma((n * drafts * SEGS,)), dma((2 * drafts * SEGS,)), dma((2 * drafts * SEGS,)),
                 dma((n,)), dma((n,)), dma((2 * n,)), dma((2 * n,)),
-                dma((8,)), dma((2,)),
+                dma((8,)), dma((2,)), dma((n * SEGS,)),
             ],
             compiler_params=pltpu.CompilerParams(
                 collective_id=0, has_side_effects=True, vmem_limit_bytes=40 * 2**20

time: 97.7 us -> 93.9 us (0.961)
  Pallas kernels: 97 us -> 93.1 us
    pallas_call x1, Pallas kernels: 91.8 us -> 88 us  [local(): pl.pallas_call(functools.partial(kernel, n), out_shape=(jax.ShapeDtypeStr...]
where the time goes in v11:
time: 93.9 us; the launch traced here: 93.8 us
  Pallas kernels  93.1 us (99%)
    pallas_call x1, Pallas kernels, local(): pl.pallas_call(functools.partial(kernel, n), out_shape=(jax.ShapeDtypeStr...  88 us
    pallas_call x1, Pallas kernels, local(): pl.pallas_call(functools.partial(finish, n), out_shape=(jax.ShapeDtypeStr...  5.17 us

profile of v11, /device:TPU:113, one launch (start us, length us, event | category | flops | bytes accessed | tf_op | source)
XLA Modules:
  0.0 93.8 jit_solution(15290740813052378129)
XLA Ops:
  0.6 88.0 %shard_map.75 = (f32[3,4096,256]{2,1,0:T(8,128)S(1)}, f32[8,256]{1,0:T(8,128)S(1)}) custom-call(s32[2,256]{1,0:T(2,128)} %bitcast.15, bf16[3,32,4096]{2,1,0:T(8,128)(2,1)} %bitcast.14, bf16[4000,4096]{1,0:T(8,128)(2,1)} %bitcast.12, f32[16000,128]{1,0:T(8,128)} %bitcast.13), custom_call_target="tpu_custom_call" | custom-call | tf_op jit(solution)/shard_map/pallas_call | solution.py:462
  88.6 5.2 %shard_map.76 = (f32[2,4000,256]{2,1,0:T(8,128)}, f32[4000,256]{1,0:T(8,128)}, f32[2,256]{1,0:T(2,128)}, f32[1,256]{1,0:T(1,128)}) custom-call(f32[3,4096,256]{2,1,0:T(8,128)S(1)} %get-tuple-element.10.z, f32[8,256]{1,0:T(8,128)S(1)} %get-tuple-element.11.small), custom_call_target="tpu_custom_call" | custom-call | tf_op jit(solution)/shard_map/pallas_call | solution.py:490

commit v12 on v7

--- a/solution.py
+++ b/solution.py
@@ -202,8 +202,11 @@
             q_send.at[slot * units + i * SEGS + s], q_recv.at[k * units + i * SEGS + s], who,
         )
 
+    def core_of(way):
+        return c if way == 0 else 1 - c
+
     def out_far(way, v):
-        i, s, cc = v // SEGS, 2 * ((v // 2) % (SEGS // 2)) + way, v % 2
+        i, s, cc = v // SEGS, v % SEGS, core_of(way)
         who = 2 * (right if way == 0 else left) + c
         return remote(
             unit(scode.at[cc], i, s), rbuf.at[way, v],
@@ -211,7 +214,7 @@
         )
 
     def relay(way, v):
-        i, s, cc = v // SEGS, 2 * ((v // 2) % (SEGS // 2)) + way, v % 2
+        i, s, cc = v // SEGS, v % SEGS, core_of(way)
         src = 2 * (left if way == 0 else right) + c
         who = 2 * (right if way == 0 else left) + cc
         return remote(

time: 92.5 us -> 92.5 us (level)
  no operation moved by 1% of the time
where the time goes in v12:
time: 92.5 us; the launch traced here: 92.4 us
  Pallas kernels  91.8 us (99%)
    pallas_call x1, Pallas kernels, local(): pl.pallas_call(functools.partial(kernel, n), out_shape=(jax.ShapeDtypeStr...  86.6 us
    pallas_call x1, Pallas kernels, local(): pl.pallas_call(functools.partial(finish, n), out_shape=(jax.ShapeDtypeStr...  5.17 us

profile of v12, /device:TPU:113, one launch (start us, length us, event | category | flops | bytes accessed | tf_op | source)
XLA Modules:
  0.0 92.4 jit_solution(9638043081646624040)
XLA Ops:
  0.6 86.6 %shard_map.75 = (f32[3,4096,256]{2,1,0:T(8,128)S(1)}, f32[8,256]{1,0:T(8,128)S(1)}) custom-call(s32[2,256]{1,0:T(2,128)} %bitcast.15, bf16[3,32,4096]{2,1,0:T(8,128)(2,1)} %bitcast.14, bf16[4000,4096]{1,0:T(8,128)(2,1)} %bitcast.12, f32[16000,128]{1,0:T(8,128)} %bitcast.13), custom_call_target="tpu_custom_call" | custom-call | tf_op jit(solution)/shard_map/pallas_call | solution.py:464
  87.2 5.2 %shard_map.76 = (f32[2,4000,256]{2,1,0:T(8,128)}, f32[4000,256]{1,0:T(8,128)}, f32[2,256]{1,0:T(2,128)}, f32[1,256]{1,0:T(1,128)}) custom-call(f32[3,4096,256]{2,1,0:T(8,128)S(1)} %get-tuple-element.10.z, f32[8,256]{1,0:T(8,128)S(1)} %get-tuple-element.11.small), custom_call_target="tpu_custom_call" | custom-call | tf_op jit(solution)/shard_map/pallas_call | solution.py:492

commit v13 on v12

--- a/solution.py
+++ b/solution.py
@@ -290,10 +290,10 @@
             for e in range(SEGS // 2):
                 send_far(SEGS + (SEGS // 2) * (t - 4) + e)
 
-        @pl.when(t >= 6)
+        @pl.when((t == 6) | (t == 8))
         def _():
             for e in range(SEGS // 2):
-                send_near(2 * SEGS + (SEGS // 2) * (t - 6) + e)
+                send_near(2 * SEGS + (SEGS // 2) * ((t - 6) // 2) + e)
 
         w_cp(t, slot).wait()
         prod = INV_TEMP * lax.dot_general(
@@ -342,6 +342,8 @@
     for p in range(1, n):
         msg(p, k).start()
 
+    for u in range(3 * SEGS, 4 * SEGS):
+        send_near(u)
     for v in range(SEGS, 2 * SEGS):
         pass_on(v)
     for p in range(1, n):

time: 92.5 us -> 92.8 us (level)
  no operation moved by 1% of the time
where the time goes in v13:
time: 92.8 us; the launch traced here: 92.7 us
  Pallas kernels  92 us (99%)
    pallas_call x1, Pallas kernels, local(): pl.pallas_call(functools.partial(kernel, n), out_shape=(jax.ShapeDtypeStr...  86.9 us
    pallas_call x1, Pallas kernels, local(): pl.pallas_call(functools.partial(finish, n), out_shape=(jax.ShapeDtypeStr...  5.17 us

profile of v13, /device:TPU:113, one launch (start us, length us, event | category | flops | bytes accessed | tf_op | source)
XLA Modules:
  0.0 92.7 jit_solution(9319669363522549007)
XLA Ops:
  0.6 86.9 %shard_map.75 = (f32[3,4096,256]{2,1,0:T(8,128)S(1)}, f32[8,256]{1,0:T(8,128)S(1)}) custom-call(s32[2,256]{1,0:T(2,128)} %bitcast.15, bf16[3,32,4096]{2,1,0:T(8,128)(2,1)} %bitcast.14, bf16[4000,4096]{1,0:T(8,128)(2,1)} %bitcast.12, f32[16000,128]{1,0:T(8,128)} %bitcast.13), custom_call_target="tpu_custom_call" | custom-call | tf_op jit(solution)/shard_map/pallas_call | solution.py:466
  87.5 5.2 %shard_map.76 = (f32[2,4000,256]{2,1,0:T(8,128)}, f32[4000,256]{1,0:T(8,128)}, f32[2,256]{1,0:T(2,128)}, f32[1,256]{1,0:T(1,128)}) custom-call(f32[3,4096,256]{2,1,0:T(8,128)S(1)} %get-tuple-element.10.z, f32[8,256]{1,0:T(8,128)S(1)} %get-tuple-element.11.small), custom_call_target="tpu_custom_call" | custom-call | tf_op jit(solution)/shard_map/pallas_call | solution.py:494

commit v14 on v12

--- a/solution.py
+++ b/solution.py
@@ -174,6 +174,62 @@
     encode(2 * far, to_slot(0))
     encode(2 * far + 1, to_slot(1))
 
+    def unit(buf_i, i, s):
+        return buf_i.at[i, s]
+
+    def landing(src, i, s):
+        return qall.at[i, s, pl.ds(pl.multiple_of(src * rows, rows), rows)]
+
+    def direct(slot, i, s, who):
+        return remote(
+            unit(scode.at[slot], i, s), landing(k, i, s),
+            q_send.at[slot * units + i * SEGS + s], q_recv.at[k * units + i * SEGS + s], who,
+        )
+
+    def core_of(way):
+        return c if way == 0 else 1 - c
+
+    def out_far(way, v):
+        i, s, cc = v // SEGS, v % SEGS, core_of(way)
+        who = 2 * (right if way == 0 else left) + c
+        return remote(
+            unit(scode.at[cc], i, s), rbuf.at[way, v],
+            q_send.at[cc * units + i * SEGS + s], r_recv.at[way * units + v], who,
+        )
+
+    def relay(way, v):
+        i, s, cc = v // SEGS, v % SEGS, core_of(way)
+        src = 2 * (left if way == 0 else right) + c
+        who = 2 * (right if way == 0 else left) + cc
+        return remote(
+            rbuf.at[way, v], landing(src, i, s),
+            r_send.at[way * units + v], q_recv.at[src * units + i * SEGS + s], who,
+        )
+
+    def near(way, u):
+        i, s, cc = u // (2 * SEGS), (u // 2) % SEGS, u % 2
+        who = 2 * (right if way == 0 else left) + cc
+        return direct(2 + 2 * way + cc, i, s, who)
+
+    def send_far(v):
+        out_far(0, v).start()
+        out_far(1, v).start()
+
+    def send_near(u):
+        near(0, u).start()
+        near(1, u).start()
+
+    def pass_on(v):
+        for way in range(2):
+            out_far(way, v).wait_recv()
+            relay(way, v).start()
+
+    def first_far(v, _):
+        send_far(v)
+        return 0
+
+    lax.fori_loop(0, SEGS, first_far, 0)
+
     fwd = []
 
     def forward(src, half):
@@ -190,56 +246,6 @@
     rel_l.start()
     forward(2 * right + c, 1)
 
-    def unit(buf_i, i, s):
-        return buf_i.at[i, s]
-
-    def landing(src, i, s):
-        return qall.at[i, s, pl.ds(pl.multiple_of(src * rows, rows), rows)]
-
-    def direct(slot, i, s, who):
-        return remote(
-            unit(scode.at[slot], i, s), landing(k, i, s),
-            q_send.at[slot * units + i * SEGS + s], q_recv.at[k * units + i * SEGS + s], who,
-        )
-
-    def core_of(way):
-        return c if way == 0 else 1 - c
-
-    def out_far(way, v):
-        i, s, cc = v // SEGS, v % SEGS, core_of(way)
-        who = 2 * (right if way == 0 else left) + c
-        return remote(
-            unit(scode.at[cc], i, s), rbuf.at[way, v],
-            q_send.at[cc * units + i * SEGS + s], r_recv.at[way * units + v], who,
-        )
-
-    def relay(way, v):
-        i, s, cc = v // SEGS, v % SEGS, core_of(way)
-        src = 2 * (left if way == 0 else right) + c
-        who = 2 * (right if way == 0 else left) + cc
-        return remote(
-            rbuf.at[way, v], landing(src, i, s),
-            r_send.at[way * units + v], q_recv.at[src * units + i * SEGS + s], who,
-        )
-
-    def near(way, u):
-        i, s, cc = u // (2 * SEGS), (u // 2) % SEGS, u % 2
-        who = 2 * (right if way == 0 else left) + cc
-        return direct(2 + 2 * way + cc, i, s, who)
-
-    def send_far(v):
-        out_far(0, v).start()
-        out_far(1, v).start()
-
-    def send_near(u):
-        near(0, u).start()
-        near(1, u).start()
-
-    def pass_on(v):
-        for way in range(2):
-            out_far(way, v).wait_recv()
-            relay(way, v).start()
-
     encode(2 * right, to_slot(2))
     encode(2 * right + 1, to_slot(3))
     encode(2 * left, to_slot(4))
@@ -250,15 +256,10 @@
     hwait(2 * right + c, 0)
     forward(2 * right + c, 0)
 
-    def first_far(v, _):
-        send_far(v)
-        return 0
-
     def first_near(u, _):
         send_near(u)
         return 0
 
-    lax.fori_loop(0, SEGS, first_far, 0)
     lax.fori_loop(0, 2 * SEGS, first_near, 0)
     encode(mate, to_slot(6))
     encode(k, to_self)
@@ -425,12 +426,15 @@
             xmsg(p, i, k).wait_send()
 
 
-def finish(n, z, small, res_ref, bonus_ref, acc_ref, exp_ref, buf, sem):
+def finish(n, z, small, res_ref, bonus_ref, acc_out, exp_out, buf, acc_ref, exp_ref, sem):
     drafts, vocab, _ = res_ref.shape
     off = pl.multiple_of((lax.axis_index("tp") * vocab) % LANES, 8)
     last = pltpu.make_async_copy(z.at[drafts, pl.ds(off, vocab), :], bonus_ref, sem.at[0])
     last.start()
     copies = [last]
+    accept = jnp.minimum(small[2:4, :] / small[4:6, :], 1.0)
+    acc_ref[...] = accept
+    exp_ref[...] = accept[0:1] + accept[0:1] * accept[1:2]
     part = vocab // PARTS
     for i in range(drafts):
         scale = small[i:i + 1, :]
@@ -440,9 +444,11 @@
             cp = pltpu.make_async_copy(buf.at[i, to], res_ref.at[i, to], sem.at[len(copies)])
             cp.start()
             copies.append(cp)
-    accept = jnp.minimum(small[2:4, :] / small[4:6, :], 1.0)
-    acc_ref[...] = accept
-    exp_ref[...] = accept[0:1] + accept[0:1] * accept[1:2]
+        if i == 0:
+            for src, dst in ((acc_ref, acc_out), (exp_ref, exp_out)):
+                cp = pltpu.make_async_copy(src, dst, sem.at[len(copies)])
+                cp.start()
+                copies.append(cp)
     for cp in copies:
         cp.wait()
 
@@ -498,8 +504,13 @@
                 jax.ShapeDtypeStruct((1, batch), F32),
             ),
             in_specs=[vmem, vmem],
-            out_specs=(anywhere, anywhere, vmem, vmem),
-            scratch_shapes=[pltpu.VMEM((drafts, vocab, batch), F32), dma((drafts * PARTS + 1,))],
+            out_specs=(anywhere,) * 4,
+            scratch_shapes=[
+                pltpu.VMEM((drafts, vocab, batch), F32),
+                pltpu.VMEM((drafts, batch), F32),
+                pltpu.VMEM((1, batch), F32),
+                dma((drafts * PARTS + 3,)),
+            ],
             compiler_params=pltpu.CompilerParams(vmem_limit_bytes=24 * 2**20),
         )(z, small)
         return accept.T, expected[0], residual.transpose(2, 0, 1), bonus.T

time: 92.5 us -> 93.8 us (1.014)
  Pallas kernels: 91.8 us -> 93.1 us
    pallas_call x1, Pallas kernels: 86.6 us -> 88.5 us  [local(): pl.pallas_call(functools.partial(kernel, n), out_shape=(jax.ShapeDtypeStr...]
where the time goes in v14:
time: 93.8 us; the launch traced here: 93.7 us
  Pallas kernels  93.1 us (99%)
    pallas_call x1, Pallas kernels, local(): pl.pallas_call(functools.partial(kernel, n), out_shape=(jax.ShapeDtypeStr...  88.5 us
    pallas_call x1, Pallas kernels, local(): pl.pallas_call(functools.partial(finish, n), out_shape=(jax.ShapeDtypeStr...  4.62 us

profile of v14, /device:TPU:113, one launch (start us, length us, event | category | flops | bytes accessed | tf_op | source)
XLA Modules:
  0.0 93.7 jit_solution(6567235960655693444)
XLA Ops:
  0.6 88.5 %shard_map.75 = (f32[3,4096,256]{2,1,0:T(8,128)S(1)}, f32[8,256]{1,0:T(8,128)S(1)}) custom-call(s32[2,256]{1,0:T(2,128)} %bitcast.15, bf16[3,32,4096]{2,1,0:T(8,128)(2,1)} %bitcast.14, bf16[4000,4096]{1,0:T(8,128)(2,1)} %bitcast.12, f32[16000,128]{1,0:T(8,128)} %bitcast.13), custom_call_target="tpu_custom_call" | custom-call | tf_op jit(solution)/shard_map/pallas_call | solution.py:470
  89.1 4.6 %shard_map.76 = (f32[2,4000,256]{2,1,0:T(8,128)}, f32[4000,256]{1,0:T(8,128)}, f32[2,256]{1,0:T(2,128)}, f32[1,256]{1,0:T(1,128)}) custom-call(f32[3,4096,256]{2,1,0:T(8,128)S(1)} %get-tuple-element.10.z, f32[8,256]{1,0:T(8,128)S(1)} %get-tuple-element.11.small), custom_call_target="tpu_custom_call" | custom-call | tf_op jit(solution)/shard_map/pallas_call | solution.py:498

commit v15 on v12

--- a/solution.py
+++ b/solution.py
@@ -425,13 +425,19 @@
             xmsg(p, i, k).wait_send()
 
 
-def finish(n, z, small, res_ref, bonus_ref, acc_ref, exp_ref, buf, sem):
+def finish(n, z, small, res_ref, bonus_ref, acc_out, exp_out, buf, acc_ref, exp_ref, sem):
     drafts, vocab, _ = res_ref.shape
     off = pl.multiple_of((lax.axis_index("tp") * vocab) % LANES, 8)
-    last = pltpu.make_async_copy(z.at[drafts, pl.ds(off, vocab), :], bonus_ref, sem.at[0])
-    last.start()
-    copies = [last]
     part = vocab // PARTS
+    copies = []
+    for t in range(PARTS):
+        at = pl.ds(pl.multiple_of(off + t * part, 8), part)
+        cp = pltpu.make_async_copy(z.at[drafts, at, :], bonus_ref.at[pl.ds(t * part, part)], sem.at[t])
+        cp.start()
+        copies.append(cp)
+    accept = jnp.minimum(small[2:4, :] / small[4:6, :], 1.0)
+    acc_ref[...] = accept
+    exp_ref[...] = accept[0:1] + accept[0:1] * accept[1:2]
     for i in range(drafts):
         scale = small[i:i + 1, :]
         for t in range(PARTS):
@@ -440,9 +446,11 @@
             cp = pltpu.make_async_copy(buf.at[i, to], res_ref.at[i, to], sem.at[len(copies)])
             cp.start()
             copies.append(cp)
-    accept = jnp.minimum(small[2:4, :] / small[4:6, :], 1.0)
-    acc_ref[...] = accept
-    exp_ref[...] = accept[0:1] + accept[0:1] * accept[1:2]
+        if i == 0:
+            for src, dst in ((acc_ref, acc_out), (exp_ref, exp_out)):
+                cp = pltpu.make_async_copy(src, dst, sem.at[len(copies)])
+                cp.start()
+                copies.append(cp)
     for cp in copies:
         cp.wait()
 
@@ -498,8 +506,13 @@
                 jax.ShapeDtypeStruct((1, batch), F32),
             ),
             in_specs=[vmem, vmem],
-            out_specs=(anywhere, anywhere, vmem, vmem),
-            scratch_shapes=[pltpu.VMEM((drafts, vocab, batch), F32), dma((drafts * PARTS + 1,))],
+            out_specs=(anywhere,) * 4,
+            scratch_shapes=[
+                pltpu.VMEM((drafts, vocab, batch), F32),
+                pltpu.VMEM((drafts, batch), F32),
+                pltpu.VMEM((1, batch), F32),
+                dma(((drafts + 1) * PARTS + 2,)),
+            ],
             compiler_params=pltpu.CompilerParams(vmem_limit_bytes=24 * 2**20),
         )(z, small)
         return accept.T, expected[0], residual.transpose(2, 0, 1), bonus.T

time: 92.5 us -> 92 us (level)
  no operation moved by 1% of the time
where the time goes in v15:
time: 92 us; the launch traced here: 91.9 us
  Pallas kernels  91.3 us (99%)
    pallas_call x1, Pallas kernels, local(): pl.pallas_call(functools.partial(kernel, n), out_shape=(jax.ShapeDtypeStr...  86.6 us
    pallas_call x1, Pallas kernels, local(): pl.pallas_call(functools.partial(finish, n), out_shape=(jax.ShapeDtypeStr...  4.65 us

profile of v15, /device:TPU:113, one launch (start us, length us, event | category | flops | bytes accessed | tf_op | source)
XLA Modules:
  0.0 91.9 jit_solution(5622732832608449367)
XLA Ops:
  0.6 86.6 %shard_map.75 = (f32[3,4096,256]{2,1,0:T(8,128)S(1)}, f32[8,256]{1,0:T(8,128)S(1)}) custom-call(s32[2,256]{1,0:T(2,128)} %bitcast.15, bf16[3,32,4096]{2,1,0:T(8,128)(2,1)} %bitcast.14, bf16[4000,4096]{1,0:T(8,128)(2,1)} %bitcast.12, f32[16000,128]{1,0:T(8,128)} %bitcast.13), custom_call_target="tpu_custom_call" | custom-call | tf_op jit(solution)/shard_map/pallas_call | solution.py:472
  87.2 4.7 %shard_map.76 = (f32[2,4000,256]{2,1,0:T(8,128)}, f32[4000,256]{1,0:T(8,128)}, f32[2,256]{1,0:T(2,128)}, f32[1,256]{1,0:T(1,128)}) custom-call(f32[3,4096,256]{2,1,0:T(8,128)S(1)} %get-tuple-element.10.z, f32[8,256]{1,0:T(8,128)S(1)} %get-tuple-element.11.small), custom_call_target="tpu_custom_call" | custom-call | tf_op jit(solution)/shard_map/pallas_call | solution.py:500

commit v16 on v15

--- a/solution.py
+++ b/solution.py
@@ -196,10 +196,13 @@
     def landing(src, i, s):
         return qall.at[i, s, pl.ds(pl.multiple_of(src * rows, rows), rows)]
 
-    def direct(slot, i, s, who):
+    def whole(src, i):
+        return qall.at[i, :, pl.ds(pl.multiple_of(src * rows, rows), rows)]
+
+    def direct(slot, i, who):
         return remote(
-            unit(scode.at[slot], i, s), landing(k, i, s),
-            q_send.at[slot * units + i * SEGS + s], q_recv.at[k * units + i * SEGS + s], who,
+            scode.at[slot, i], whole(k, i),
+            q_send.at[slot * units + i * SEGS], q_recv.at[k * units + i * SEGS], who,
         )
 
     def core_of(way):
@@ -222,18 +225,13 @@
             r_send.at[way * units + v], q_recv.at[src * units + i * SEGS + s], who,
         )
 
-    def near(way, u):
-        i, s, cc = u // (2 * SEGS), (u // 2) % SEGS, u % 2
-        who = 2 * (right if way == 0 else left) + cc
-        return direct(2 + 2 * way + cc, i, s, who)
-
     def send_far(v):
         out_far(0, v).start()
         out_far(1, v).start()
 
-    def send_near(u):
-        near(0, u).start()
-        near(1, u).start()
+    def send_near(i, cc):
+        direct(2 + cc, i, 2 * right + cc).start()
+        direct(4 + cc, i, 2 * left + cc).start()
 
     def pass_on(v):
         for way in range(2):
@@ -254,20 +252,13 @@
         send_far(v)
         return 0
 
-    def first_near(u, _):
-        send_near(u)
-        return 0
-
     lax.fori_loop(0, SEGS, first_far, 0)
-    lax.fori_loop(0, 2 * SEGS, first_near, 0)
+    send_near(0, c)
     encode(mate, to_slot(6))
     encode(k, to_self)
 
-    def to_mate(u, _):
-        direct(6, u // SEGS, u % SEGS, mate).start()
-        return 0
-
-    lax.fori_loop(0, drafts * SEGS, to_mate, 0)
+    for i in range(drafts):
+        direct(6, i, mate).start()
 
     hwait(2 * far + c, 0)
     forward(2 * far + c, 0)
@@ -290,10 +281,9 @@
             for e in range(SEGS // 2):
                 send_far(SEGS + (SEGS // 2) * (t - 4) + e)
 
-        @pl.when(t >= 6)
-        def _():
-            for e in range(SEGS // 2):
-                send_near(2 * SEGS + (SEGS // 2) * (t - 6) + e)
+        pl.when(t == 1)(lambda: send_near(0, 1 - c))
+        pl.when(t == 6)(lambda: send_near(1, c))
+        pl.when(t == 8)(lambda: send_near(1, 1 - c))
 
         w_cp(t, slot).wait()
         prod = INV_TEMP * lax.dot_general(
@@ -366,10 +356,6 @@
     def xmsg(p, i, src):
         return remote(mass.at[i, src], mass.at[i, src], x_send.at[i * n + p], x_recv.at[i * n + src], (k + p) % n)
 
-    def drain(u, _):
-        direct(u // units, (u % units) // SEGS, u % SEGS, mate).wait_send()
-        return 0
-
     def drain_relay(v, _):
         relay(0, v).wait_send()
         relay(1, v).wait_send()
@@ -377,15 +363,21 @@
 
     for i in range(drafts):
         acc = [jnp.zeros((8, LANES), F32) for _ in range(batch // LANES)]
+        for src in (2 * left, 2 * left + 1, 2 * right, 2 * right + 1, mate):
+            remote(whole(src, i), whole(src, i), q_send.at[0], q_recv.at[src * units + i * SEGS], mate).wait_recv()
         for s in range(SEGS):
             if i == drafts - 1 and s == SEGS - 1:
                 for cp in own_sends + [rel_r, rel_l] + fwd:
                     cp.wait_send()
                 for p in range(1, n):
                     msg(p, k).wait_send()
-                lax.fori_loop(0, (n - 1) * units, drain, 0)
-            for p in range(1, n):
-                src = (k + p) % n
+                for v in range(units):
+                    for way in range(2):
+                        out_far(way, v).wait_send()
+                for slot in range(2, n - 1):
+                    for ii in range(drafts):
+                        direct(slot, ii, mate).wait_send()
+            for src in (2 * far, 2 * far + 1):
                 remote(
                     landing(src, i, s), landing(src, i, s), q_send.at[0],
                     q_recv.at[src * units + i * SEGS + s], mate,
@@ -429,12 +421,9 @@
     drafts, vocab, _ = res_ref.shape
     off = pl.multiple_of((lax.axis_index("tp") * vocab) % LANES, 8)
     part = vocab // PARTS
-    copies = []
-    for t in range(PARTS):
-        at = pl.ds(pl.multiple_of(off + t * part, 8), part)
-        cp = pltpu.make_async_copy(z.at[drafts, at, :], bonus_ref.at[pl.ds(t * part, part)], sem.at[t])
-        cp.start()
-        copies.append(cp)
+    last = pltpu.make_async_copy(z.at[drafts, pl.ds(off, vocab), :], bonus_ref, sem.at[0])
+    last.start()
+    copies = [last]
     accept = jnp.minimum(small[2:4, :] / small[4:6, :], 1.0)
     acc_ref[...] = accept
     exp_ref[...] = accept[0:1] + accept[0:1] * accept[1:2]

time: 92 us -> 91.4 us (level)
  no operation moved by 1% of the time
where the time goes in v16:
time: 91.4 us
  Pallas kernels  90.7 us (99%)
    pallas_call x1, Pallas kernels, local(): pl.pallas_call(functools.partial(kernel, n), out_shape=(jax.ShapeDtypeStr...  86.1 us
    pallas_call x1, Pallas kernels, local(): pl.pallas_call(functools.partial(finish, n), out_shape=(jax.ShapeDtypeStr...  4.65 us

profile of v16, /device:TPU:113, one launch (start us, length us, event | category | flops | bytes accessed | tf_op | source)
XLA Modules:
  0.0 91.4 jit_solution(4717381337909405279)
XLA Ops:
  0.6 86.1 %shard_map.75 = (f32[3,4096,256]{2,1,0:T(8,128)S(1)}, f32[8,256]{1,0:T(8,128)S(1)}) custom-call(s32[2,256]{1,0:T(2,128)} %bitcast.15, bf16[3,32,4096]{2,1,0:T(8,128)(2,1)} %bitcast.14, bf16[4000,4096]{1,0:T(8,128)(2,1)} %bitcast.12, f32[16000,128]{1,0:T(8,128)} %bitcast.13), custom_call_target="tpu_custom_call" | custom-call | tf_op jit(solution)/shard_map/pallas_call | solution.py:461
  86.7 4.7 %shard_map.76 = (f32[2,4000,256]{2,1,0:T(8,128)}, f32[4000,256]{1,0:T(8,128)}, f32[2,256]{1,0:T(2,128)}, f32[1,256]{1,0:T(1,128)}) custom-call(f32[3,4096,256]{2,1,0:T(8,128)S(1)} %get-tuple-element.10.z, f32[8,256]{1,0:T(8,128)S(1)} %get-tuple-element.11.small), custom_call_target="tpu_custom_call" | custom-call | tf_op jit(solution)/shard_map/pallas_call | solution.py:489

commit v17 on v16

--- a/solution.py
+++ b/solution.py
@@ -84,11 +84,11 @@
     hid_cp.wait()
     own_sends = []
     for idx, (who, half) in enumerate(
-        [(2 * right + c, 0), (2 * left + c, 1), (2 * right + c, 1), (2 * left + c, 0), (mate, 0), (mate, 1)]
+        [(2 * right + c, 0), (2 * left + c, 1), (mate, 0), (mate, 1), (2 * right + c, 1), (2 * left + c, 0)]
     ):
-        cp = hcopy(k, half, h_send.at[idx], who)
+        own_sends.append(hcopy(k, half, h_send.at[idx], who))
+    for cp in own_sends[:4]:
         cp.start()
-        own_sends.append(cp)
     for g in range(rows // 8):
         stage_cp(g).start()
     w_cp(0, 0).start()
@@ -181,6 +181,9 @@
         cp.start()
         fwd.append(cp)
 
+    for way in range(2):
+        own_sends[way].wait_send()
+        own_sends[4 + way].start()
     hwait(2 * left + c, 0)
     rel_r = hcopy(2 * left + c, 0, h_send.at[6], 2 * right + c)
     rel_r.start()
@@ -367,7 +370,7 @@
             remote(whole(src, i), whole(src, i), q_send.at[0], q_recv.at[src * units + i * SEGS], mate).wait_recv()
         for s in range(SEGS):
             if i == drafts - 1 and s == SEGS - 1:
-                for cp in own_sends + [rel_r, rel_l] + fwd:
+                for cp in own_sends[2:] + [rel_r, rel_l] + fwd:
                     cp.wait_send()
                 for p in range(1, n):
                     msg(p, k).wait_send()

time: 91.4 us -> 92 us (level)
  no operation moved by 1% of the time
where the time goes in v17:
time: 92 us; the launch traced here: 91.9 us
  Pallas kernels  91.3 us (99%)
    pallas_call x1, Pallas kernels, local(): pl.pallas_call(functools.partial(kernel, n), out_shape=(jax.ShapeDtypeStr...  86.6 us
    pallas_call x1, Pallas kernels, local(): pl.pallas_call(functools.partial(finish, n), out_shape=(jax.ShapeDtypeStr...  4.65 us

profile of v17, /device:TPU:113, one launch (start us, length us, event | category | flops | bytes accessed | tf_op | source)
XLA Modules:
  0.0 91.9 jit_solution(8259221370844951862)
XLA Ops:
  0.6 86.6 %shard_map.75 = (f32[3,4096,256]{2,1,0:T(8,128)S(1)}, f32[8,256]{1,0:T(8,128)S(1)}) custom-call(s32[2,256]{1,0:T(2,128)} %bitcast.15, bf16[3,32,4096]{2,1,0:T(8,128)(2,1)} %bitcast.14, bf16[4000,4096]{1,0:T(8,128)(2,1)} %bitcast.12, f32[16000,128]{1,0:T(8,128)} %bitcast.13), custom_call_target="tpu_custom_call" | custom-call | tf_op jit(solution)/shard_map/pallas_call | solution.py:464
  87.3 4.7 %shard_map.76 = (f32[2,4000,256]{2,1,0:T(8,128)}, f32[4000,256]{1,0:T(8,128)}, f32[2,256]{1,0:T(2,128)}, f32[1,256]{1,0:T(1,128)}) custom-call(f32[3,4096,256]{2,1,0:T(8,128)S(1)} %get-tuple-element.10.z, f32[8,256]{1,0:T(8,128)S(1)} %get-tuple-element.11.small), custom_call_target="tpu_custom_call" | custom-call | tf_op jit(solution)/shard_map/pallas_call | solution.py:492
